TPU v7x, 32 devices: a whole 2x2x4 slice. The times are simulated.
32 devices in a mesh: row: 4 (over x, core), col: 4 (over z), depth: 2 (over y).
Axes of the slice: x: 2, y: 2, z: 4, core: 2. Of those that a mesh axis runs over, the one named last changes fastest.
Arguments:
- acts: bfloat16 [256, 32768], P('depth', 'row'), may hold values from -6 to 6
- act_mask: int32 [256, 256], P('depth', 'row'), may hold values 0 or 1
- w1: bfloat16 [256, 32, 128, 128], P(('row', 'depth'), 'col'), may hold values from -0.09375 to 0.09375
- cols1: int32 [256, 32], P('row', 'col'), may hold values from 0 to 255, as said below
- bias1: float32 [32768], P('col'), may hold values from -3 to 3
- mask2: int32 [256, 256], P('depth', 'col'), may hold values 0 or 1
- w2: bfloat16 [256, 32, 128, 128], P(('col', 'depth'), 'row'), may hold values from -0.1875 to 0.1875
- cols2: int32 [256, 32], P('col', 'row'), may hold values from 0 to 255, as said below
- bias2: float32 [32768], P(('row', 'col')), may hold values from -3 to 3
Outputs:
- result: bfloat16 [256, 32768], P('depth', ('row', 'col'))
Inputs may be any that keep to these rules, and one draw needn't show every extreme that they name: `cols1`: in each of the 256 block rows the 32 entries name different block columns, and for every g the entries g * 8 to g * 8 + 7 lie among block columns g * 64 to g * 64 + 63. `cols2`: in each of the 256 block rows the 32 entries name different block columns, and for every g the entries g * 8 to g * 8 + 7 lie among block columns g * 64 to g * 64 + 63.
All inputs are finite; a program needn't handle non-finite values. No bound on the sum of `act_mask` or of `mask2` on one device may be relied on, other than what follows from the above.
Results may differ from a plain program's by a relative error of at most 0.0047.
Values may be sent and summed in bfloat16 or wider, within the bound.
A program may use at most 128 MiB of HBM per device.

v0:
```python
import functools

import jax
import jax.numpy as jnp
from jax import lax
from jax.experimental import pallas as pl
from jax.experimental.pallas import tpu as pltpu
from jax.sharding import PartitionSpec as P


def fold_function(inputs, targets, stride):

    def add_tiles(running_total, tiles, first_row):

        def advance(number, total):
            offset = number * stride
            block_list = lax.dynamic_slice_in_dim(tiles, offset, stride, 0)
            incoming_rows = lax.dynamic_slice_in_dim(inputs, offset, stride, 1)
            wanted = lax.dynamic_slice_in_dim(targets, offset, stride, 0)
            product = jnp.einsum(
                "tws,wish->twih", incoming_rows, block_list, preferred_element_type=jnp.float32
            )
            flat_product = product.reshape(product.shape[0], -1, product.shape[-1])
            return total.at[:, wanted.reshape(-1)].add(flat_product)

        return lax.fori_loop(0, tiles.shape[0] // stride, advance, running_total)

    return add_tiles


def gathered_weights(acts, act_mask, w1, cols1, bias1, mask2, w2, cols2, bias2):
    block = w1.shape[-1]
    rows_dev = acts.shape[0]
    row_blocks = act_mask.shape[1]
    col_blocks = mask2.shape[1]
    row_index = lax.axis_index("row")
    col_index = lax.axis_index("col")
    masked = acts.reshape(rows_dev, row_blocks, block) * act_mask[:, :, None].astype(jnp.bfloat16)
    first_layer_destinations = cols1 - col_index * col_blocks
    second_targets = cols2 - row_index * row_blocks
    first_offset_value = jnp.zeros((rows_dev, col_blocks, block), jnp.float32)
    first_fold = fold_function(masked, first_layer_destinations, w1.shape[0])
    first_sum = first_fold(
        first_offset_value, lax.all_gather(w1, "depth", axis=0, tiled=True), jnp.int32(0)
    )
    bias_blocks = bias1.reshape(col_blocks, block)
    share = col_blocks // lax.axis_size("row")
    part_sum = lax.psum_scatter(first_sum, "row", scatter_dimension=1, tiled=True)
    bias_part = lax.dynamic_slice_in_dim(bias_blocks, row_index * share, share, 0)
    mask_part = lax.dynamic_slice_in_dim(mask2, row_index * share, share, 1)
    hidden_part = jnp.maximum(part_sum + bias_part, 0.0) * mask_part[:, :, None].astype(jnp.float32)
    hidden = lax.all_gather(hidden_part.astype(jnp.bfloat16), "row", axis=1, tiled=True)
    second_start = jnp.zeros((rows_dev, row_blocks, block), jnp.float32)
    second_fold = fold_function(hidden, second_targets, w2.shape[0])
    second_sum = second_fold(
        second_start, lax.all_gather(w2, "depth", axis=0, tiled=True), jnp.int32(0)
    )
    outcome = lax.psum_scatter(second_sum, "col", scatter_dimension=1, tiled=True)
    bias_out = bias2.reshape(outcome.shape[1], block)
    return jnp.maximum(outcome + bias_out, 0.0).astype(jnp.bfloat16).reshape(rows_dev, -1)


def sparse_kernel(per_step, entries, blocked, cols_ref, core_ref, x_ref, w_ref, *refs):
    *outs, total = refs
    step = pl.program_id(0)
    block = w_ref.shape[-1]

    @pl.when(step == 0)
    def _():
        total[...] = jnp.zeros_like(total)

    for row in range(per_step):
        if blocked:
            x = x_ref[:, row].reshape(-1, block)
        else:
            x = x_ref[:, row * block:(row + 1) * block]
        for entry in range(0, entries, 2):
            pair = jnp.concatenate([w_ref[row, entry], w_ref[row, entry + 1]], axis=1)
            product = jnp.dot(x, pair, preferred_element_type=jnp.float32)
            base = (step * per_step + row) * entries + entry
            total[cols_ref[base]] += product[:, :block]
            total[cols_ref[base + 1]] += product[:, block:]

    @pl.when(step == pl.num_programs(0) - 1)
    def _():
        if blocked:
            rows = outs[0].shape[1]
            for half, out in enumerate(outs):
                out[...] = total[:, half * rows:(half + 1) * rows].astype(out.dtype)
        else:
            kept, given = outs
            pieces, size = kept.shape[:2]
            core = core_ref[0]
            for piece in range(pieces):
                start = piece * 2 * size
                kept[piece] = total[pl.ds(start + core * size, size)]
                given[piece] = total[pl.ds(start + (1 - core) * size, size)].astype(given.dtype)


def sparse_partial(x, weights, cols, core, out_blocks, blocked, outs):
    stored, entries, block, _ = weights.shape
    rows = x.shape[2] if blocked else x.shape[0]
    lines = 2 * rows if blocked else rows
    per_step = 4 if stored % 4 == 0 else 1
    if blocked:
        x_spec = pl.BlockSpec((2, per_step, rows, block), lambda i, *_: (0, i, 0, 0))
    else:
        x_spec = pl.BlockSpec((rows, per_step * block), lambda i, *_: (0, i))
    zeros = [(lambda n: lambda i, *_: (0,) * n)(len(out.shape)) for out in outs]
    return pl.pallas_call(
        functools.partial(sparse_kernel, per_step, entries, blocked),
        out_shape=outs,
        grid_spec=pltpu.PrefetchScalarGridSpec(
            num_scalar_prefetch=2,
            grid=(stored // per_step,),
            in_specs=[
                x_spec,
                pl.BlockSpec((per_step, entries, block, block), lambda i, *_: (i, 0, 0, 0)),
            ],
            out_specs=[pl.BlockSpec(out.shape, zero) for out, zero in zip(outs, zeros)],
            scratch_shapes=[pltpu.VMEM((out_blocks, lines, block), jnp.float32)],
        ),
        compiler_params=pltpu.CompilerParams(
            dimension_semantics=("arbitrary",), vmem_limit_bytes=40 * 1024 * 1024
        ),
        cost_estimate=pl.CostEstimate(
            flops=2 * lines * weights.size, bytes_accessed=2 * weights.size, transcendentals=0
        ),
    )(cols.reshape(-1), core.reshape(1), x, weights)


MESH = pl.DeviceIdType.MESH
F32, BF16 = jnp.float32, jnp.bfloat16


def greet(partners):
    barrier = pltpu.get_barrier_semaphore()
    for partner in partners:
        pl.semaphore_signal(barrier, inc=1, device_id=partner, device_id_type=MESH)
    pl.semaphore_wait(barrier, len(partners))


def first_reduce_kernel(
    chunks, kept0, kept1, given0, given1, bias, live, out,
    core_in, total, y_out, y_in, x_out, x_in, send_sem, recv_sem,
):
    r, d = lax.axis_index("row"), lax.axis_index("depth")
    x, core = r // 2, r % 2
    partner = {"row": x * 2 + 1 - core}
    y_peer = {"depth": 1 - d}
    x_peer = {"row": (1 - x) * 2 + core}
    kept, given = (kept0, kept1), (given0, given1)
    size = kept0.shape[2] // chunks
    steps = [(half, part) for part in range(chunks) for half in range(2)]
    arrivals = [(1 - half, part) for half, part in steps]
    started = []

    def send(stage, source, target, step, landing, device):
        copy = pltpu.make_async_remote_copy(
            src_ref=source, dst_ref=target,
            send_sem=send_sem.at[stage, step[0], step[1]],
            recv_sem=recv_sem.at[stage, landing[0], landing[1]],
            device_id=device, device_id_type=MESH,
        )
        copy.start()
        started.append(copy)

    def await_arrival(stage, target, step):
        pltpu.make_async_remote_copy(
            src_ref=target, dst_ref=target,
            send_sem=send_sem.at[stage, step[0], step[1]],
            recv_sem=recv_sem.at[stage, step[0], step[1]],
            device_id=x_peer, device_id_type=MESH,
        ).wait_recv()

    greet([partner, y_peer, x_peer])
    for step in steps:
        half, part = step
        cut = pl.ds(part * size, size)
        send(0, given[half].at[:, :, cut], core_in.at[half, part], step, step, partner)

    def pair(step):
        half, part = step
        cut = pl.ds(part * size, size)
        await_arrival(0, core_in.at[half, part], step)
        y_out[half, part] = (
            kept[half][1 - d, :, cut] + core_in[half, part, 1 - d].astype(F32)
        ).astype(BF16)
        send(1, y_out.at[half, part], y_in.at[1 - half, part], step, (1 - half, part), y_peer)
        total[half, part] = kept[half][d, :, cut] + core_in[half, part, d].astype(F32)

    def along_y(step):
        half, part = step
        await_arrival(1, y_in.at[half, part], step)
        x_out[half, part] = (
            total[half, part, 1 - x] + y_in[half, part, 1 - x].astype(F32)
        ).astype(BF16)
        send(2, x_out.at[half, part], x_in.at[half, part], step, step, x_peer)

    def along_x(step):
        half, part = step
        cut = pl.ds(part * size, size)
        await_arrival(2, x_in.at[half, part], step)
        z = total[half, part, x] + y_in[half, part, x].astype(F32) + x_in[half, part].astype(F32)
        for b in range(size):
            at = part * size + b
            value = jnp.maximum(z[b] + bias[at:at + 1, :], 0.0) * live[half, :, at:at + 1]
            out[half, x, core, at] = value.astype(BF16)
        mine = out.at[half, x, core, cut]
        send(3, mine, mine, step, step, x_peer)
        send(4, mine, mine, step, step, partner)

    def forward(step):
        half, part = step
        cut = pl.ds(part * size, size)
        await_arrival(3, out.at[half, 1 - x, core, cut], step)
        theirs = out.at[half, 1 - x, core, cut]
        send(5, theirs, theirs, step, step, partner)

    count = len(steps)
    for at in range(count + 3):
        if at < count:
            pair(steps[at])
        if 0 <= at - 1 < count:
            along_y(arrivals[at - 1])
        if 0 <= at - 2 < count:
            along_x(arrivals[at - 2])
        if 0 <= at - 3 < count:
            forward(arrivals[at - 3])
    for step in arrivals:
        half, part = step
        cut = pl.ds(part * size, size)
        await_arrival(4, out.at[half, x, 1 - core, cut], step)
        await_arrival(5, out.at[half, 1 - x, 1 - core, cut], step)
    for copy in started:
        copy.wait_send()


def first_reduce(kept, given, bias, live):
    _, _, share, rows, block = kept[0].shape
    chunks = 4 if share % 4 == 0 else 1
    size = share // chunks
    vmem = pl.BlockSpec(memory_space=pltpu.VMEM)
    return pl.pallas_call(
        functools.partial(first_reduce_kernel, chunks),
        out_shape=jax.ShapeDtypeStruct((2, 2, 2, share, rows, block), BF16),
        in_specs=[vmem] * 6,
        out_specs=vmem,
        scratch_shapes=[
            pltpu.VMEM((2, chunks, 2, 2, size, rows, block), BF16),
            pltpu.VMEM((2, chunks, 2, size, rows, block), F32),
            pltpu.VMEM((2, chunks, 2, size, rows, block), BF16),
            pltpu.VMEM((2, chunks, 2, size, rows, block), BF16),
            pltpu.VMEM((2, chunks, size, rows, block), BF16),
            pltpu.VMEM((2, chunks, size, rows, block), BF16),
            pltpu.SemaphoreType.DMA((6, 2, chunks)),
            pltpu.SemaphoreType.DMA((6, 2, chunks)),
        ],
        compiler_params=pltpu.CompilerParams(
            collective_id=1, has_side_effects=True, vmem_limit_bytes=48 * 1024 * 1024
        ),
        name="first_reduce",
    )(*kept, *given, bias, live)


def second_reduce_kernel(n_col, parts, home, away, bias, out, y_in, z_out, z_in, send_y, recv_y, send_z, recv_z):
    c, d = lax.axis_index("col"), lax.axis_index("depth")
    share, block = out.shape[1] // home.shape[2], home.shape[2]
    size = home.shape[1] // parts
    last = n_col - 1
    upper = c // 2
    inner = c + upper * (last - 2 * c)
    y_peer = {"depth": 1 - d}
    steps = [(i, p) for i in range(n_col) for p in range(parts)]

    def mirrored(value):
        return value + upper * (last - 2 * value)

    def owner(i):
        end, mid = (3, 2, 1, 0)[i], (2, 0, 3, 1)[i]
        return mirrored(end + inner * (mid - end))

    def receiver(i):
        end, mid = (1, 2, 1)[i], (2, 0, 3)[i]
        return mirrored(end + inner * (mid - end))

    def y_copy(i, p):
        return pltpu.make_async_remote_copy(
            src_ref=away.at[pl.ds(owner(i) * share, share), pl.ds(p * size, size)],
            dst_ref=y_in.at[i, p],
            send_sem=send_y.at[i, p], recv_sem=recv_y.at[i, p],
            device_id=y_peer, device_id_type=MESH,
        )

    def z_copy(i, p):
        slot = 3 * inner if i == 0 else i
        return pltpu.make_async_remote_copy(
            src_ref=z_out.at[i, p], dst_ref=z_in.at[slot, p],
            send_sem=send_z.at[i, p], recv_sem=recv_z.at[slot, p],
            device_id={"col": receiver(i)}, device_id_type=MESH,
        )

    def z_arrival(slot, p):
        pltpu.make_async_remote_copy(
            src_ref=z_in.at[slot, p], dst_ref=z_in.at[slot, p],
            send_sem=send_z.at[0, p], recv_sem=recv_z.at[slot, p],
            device_id={"col": receiver(0)}, device_id_type=MESH,
        ).wait_recv()

    greet([y_peer] + [{"col": lax.rem(c + o, n_col)} for o in range(1, n_col)])
    for i, p in steps:
        y_copy(i, p).start()

    def near_sum(i, p):
        return home[pl.ds(owner(i) * share, share), p * size:(p + 1) * size] + y_in[i, p].astype(F32)

    for i, p in steps[:-parts]:
        y_copy(i, p).wait_recv()
        if i == 2:
            @pl.when(inner == 1)
            def _():
                z_arrival(0, p)
                z_out[i, p] = (near_sum(i, p) + z_in[0, p].astype(F32)).astype(BF16)

            @pl.when(inner == 0)
            def _():
                z_out[i, p] = near_sum(i, p).astype(BF16)
        else:
            z_out[i, p] = near_sum(i, p).astype(BF16)
        z_copy(i, p).start()

    def finish(p, slots):
        for slot in slots:
            z_arrival(slot, p)
        for b in range(share):
            value = home[c * share + b, p * size:(p + 1) * size] + y_in[n_col - 1, p, b].astype(F32)
            for slot in slots:
                value += z_in[slot, p, b].astype(F32)
            value = jnp.maximum(value + bias[b:b + 1, :], 0.0)
            out[p * size:(p + 1) * size, b * block:(b + 1) * block] = value.astype(BF16)

    for p in range(parts):
        y_copy(n_col - 1, p).wait_recv()

        @pl.when(inner == 1)
        def _():
            finish(p, (1, 2, 3))

        @pl.when(inner == 0)
        def _():
            finish(p, (1, 2))
    for i, p in steps:
        y_copy(i, p).wait_send()
        if i < n_col - 1:
            z_copy(i, p).wait_send()


def second_reduce(home, away, bias, n_col):
    blocks, rows, block = home.shape
    share = blocks // n_col
    parts = 2
    size = rows // parts
    vmem = pl.BlockSpec(memory_space=pltpu.VMEM)
    return pl.pallas_call(
        functools.partial(second_reduce_kernel, n_col, parts),
        out_shape=jax.ShapeDtypeStruct((rows, share * block), BF16),
        in_specs=[vmem] * 3,
        out_specs=vmem,
        scratch_shapes=[
            pltpu.VMEM((n_col, parts, share, size, block), BF16),
            pltpu.VMEM((n_col - 1, parts, share, size, block), BF16),
            pltpu.VMEM((n_col, parts, share, size, block), BF16),
            pltpu.SemaphoreType.DMA((n_col, parts)),
            pltpu.SemaphoreType.DMA((n_col, parts)),
            pltpu.SemaphoreType.DMA((n_col - 1, parts)),
            pltpu.SemaphoreType.DMA((n_col, parts)),
        ],
        compiler_params=pltpu.CompilerParams(
            collective_id=2, has_side_effects=True, vmem_limit_bytes=48 * 1024 * 1024
        ),
        name="second_reduce",
    )(home, away, bias)


def exchanged_rows(acts, act_mask, w1, cols1, bias1, mask2, w2, cols2, bias2):
    block = w1.shape[-1]
    stored1, stored2 = w1.shape[0], w2.shape[0]
    rows = acts.shape[0]
    row_blocks, col_blocks = act_mask.shape[1], mask2.shape[1]
    r, c, d = lax.axis_index("row"), lax.axis_index("col"), lax.axis_index("depth")
    n_row, n_col = lax.axis_size("row"), lax.axis_size("col")
    other = 1 - d
    swap = [(0, 1), (1, 0)]
    masked = (acts.reshape(rows, row_blocks, block) * act_mask[:, :, None].astype(BF16)).reshape(rows, -1)
    keep = lax.dynamic_slice_in_dim(masked, d * stored1 * block, stored1 * block, 1)
    give = lax.dynamic_slice_in_dim(masked, other * stored1 * block, stored1 * block, 1)
    taken = lax.ppermute(give, "depth", swap)
    to1 = lax.dynamic_slice_in_dim(cols1, d * stored1, stored1, 0) - c * col_blocks
    to2 = lax.dynamic_slice_in_dim(cols2, d * stored2, stored2, 0) - r * row_blocks
    core = r % 2
    share = col_blocks // 2 // n_row
    shape1 = (col_blocks // share // 2, share, rows, block)
    outs1 = [jax.ShapeDtypeStruct(shape1, F32), jax.ShapeDtypeStruct(shape1, BF16)]
    kept0, given0 = sparse_partial(keep, w1, to1, core, col_blocks, False, outs1)
    kept1, given1 = sparse_partial(taken, w1, to1, core, col_blocks, False, outs1)
    first = d * (col_blocks // 2) + r * share
    bias_part = lax.dynamic_slice_in_dim(bias1.reshape(col_blocks, block), first, share, 0)
    live = jnp.stack([mask2.astype(F32), lax.ppermute(mask2.astype(F32), "depth", swap)])
    live = lax.dynamic_slice_in_dim(live, first, share, 2)
    split = (2, n_row // 2, share, rows, block)
    x1 = first_reduce(
        [kept0.reshape(split), kept1.reshape(split)],
        [given0.reshape(split), given1.reshape(split)],
        bias_part, live,
    ).reshape(2, col_blocks // 2, rows, block)
    shape2 = (row_blocks, rows, block)
    outs2 = [jax.ShapeDtypeStruct(shape2, F32), jax.ShapeDtypeStruct(shape2, BF16)]
    home, away = sparse_partial(x1, w2, to2, core, row_blocks, True, outs2)
    return second_reduce(home, away, bias2.reshape(row_blocks // n_col, block), n_col)


def solution(mesh):
    near = mesh.shape["depth"] == 2 and mesh.shape["row"] == 4 and mesh.shape["col"] == 4
    return jax.shard_map(
        exchanged_rows if near else gathered_weights,
        mesh=mesh,
        in_specs=(
            P("depth", "row"),
            P("depth", "row"),
            P(("row", "depth"), "col", None, None),
            P("row", "col"),
            P("col"),
            P("depth", "col"),
            P(("col", "depth"), "row", None, None),
            P("col", "row"),
            P(("row", "col")),
        ),
        out_specs=P("depth", ("row", "col")),
        check_vma=False,
    )
```

profile of v0, /device:TPU:0, one launch (start us, length us, event | category | flops | bytes accessed | tf_op | source)
XLA Modules:
  0.0 148.4 jit_solution(8769401115387340412)
XLA Ops:
  0.0 0.0 copy-start
  0.0 0.0 copy-start.7
  0.0 0.9 convert_element_type.8
  0.9 0.1 copy.14
  1.0 1.6 %mul.36 = bf16[128,64,128]{2,1,0:T(8,128)(2,1)S(1)} broadcast(bf16[128,64]{1,0:T(8,128)(2,1)S(1)} %copy.14), dimensions={0,1} | broadcast | bytes 2113536 | tf_op jit(solution)/shard_map/mul | solution.py:394
  2.7 0.0 copy-done.7
  2.7 1.3 bitcast_multiply_fusion
  4.0 0.0 copy-start.8
  4.0 0.0 copy-start.9
  4.0 0.0 copy-start.10
  4.0 1.2 constant_dynamic-slice_fusion.1
  5.2 3.0 %collective-permute-start = (bf16[128,4096]{1,0:T(8,128)(2,1)}, bf16[128,4096]{1,0:T(8,128)(2,1)S(1)}, u32[]{:S(2)}, u32[]{:S(2)}) collective-permute-start(bf16[128,4096]{1,0:T(8,128)(2,1)} %get-tuple-element.17), channel_id=1, source_target_pairs={{0,1},{1,0},{2,3},{3,2},{4,5},{5,4},{6,7},{7,6},{8,9},{9,8},{10,11... | collective-permute-start | bytes 3145736 | tf_op jit(solution)/shard_map/ppermute | solution.py:397
  8.2 0.0 copy-done.8
  8.2 0.1 copy.15
  8.3 0.1 collective-permute-start.1
  8.4 0.0 copy-done.9
  8.4 0.0 copy-done.10
  8.4 0.1 dynamic-slice_subtract_fusion
  8.5 0.1 copy.13
  8.5 0.1 reshape.40.cols_ref
  8.6 0.0 copy-done
  8.7 0.0 copy-start.1
  8.7 3.4 %copy-done.1 = bf16[32,8,128,128]{3,2,1,0:T(8,128)(2,1)S(1)} copy-done((bf16[32,8,128,128]{3,2,1,0:T(8,128)(2,1)S(1)}, bf16[32,8,128,128]{3,2,1,0:T(8,128)(2,1)}, u32[]{:S(2)}) %copy-start.1) | copy-done | bytes 8388632
  12.0 4.9 %shard_map.91 = (f32[4,8,128,128]{3,2,1,0:T(8,128)S(1)}, bf16[4,8,128,128]{3,2,1,0:T(8,128)(2,1)S(1)}) custom-call(s32[256]{0:T(256)S(1)} %reshape.40.cols_ref, s32[1]{0:T(128)} %bitcast.core_ref, bf16[128,4096]{1,0:T(8,128)(2,1)S(1)} %get-tuple-element.18.x_ref, bf16[32,8,128,128]{3,2,1,0:T(8,128)(2,1)S(1)} %copy-done.1), custom_call_target="tpu_custom_call" | custom-call | flops 1073741824 | bytes 8388608 | tf_op jit(solution)/shard_map/pallas_call | solution.py:110
  17.0 0.0 copy-start.4
  17.0 1.3 copy-done.4
  18.3 0.1 copy.12
  18.4 0.1 reshape.38.cols_ref
  18.5 14.4 %collective-permute-done.1 = f32[128,64]{1,0:T(8,128)S(1)} collective-permute-done((f32[128,64]{1,0:T(8,128)S(1)}, f32[128,64]{1,0:T(8,128)S(1)}, u32[]{:S(2)}, u32[]{:S(2)}) %collective-permute-start.1) | collective-permute-done | bytes 32800 | tf_op jit(solution)/shard_map/ppermute | solution.py:408
  32.9 0.1 dynamic-slice_maximum_fusion.live
  33.0 0.0 collective-permute-done.x_ref
  33.0 0.0 copy-start.2
  33.0 3.4 %copy-done.2 = bf16[32,8,128,128]{3,2,1,0:T(8,128)(2,1)S(1)} copy-done((bf16[32,8,128,128]{3,2,1,0:T(8,128)(2,1)S(1)}, bf16[32,8,128,128]{3,2,1,0:T(8,128)(2,1)}, u32[]{:S(2)}) %copy-start.2) | copy-done | bytes 8388632
  36.4 4.9 %shard_map.92 = (f32[4,8,128,128]{3,2,1,0:T(8,128)S(1)}, bf16[4,8,128,128]{3,2,1,0:T(8,128)(2,1)S(1)}) custom-call(s32[256]{0:T(256)S(1)} %reshape.40.cols_ref, s32[1]{0:T(128)} %bitcast.core_ref, bf16[128,4096]{1,0:T(8,128)(2,1)S(1)} %collective-permute-done.x_ref, bf16[32,8,128,128]{3,2,1,0:T(8,128)(2,1)S(1)} %copy-done.2), custom_call_target="tpu_custom_call" | custom-call | flops 1073741824 | bytes 8388608 | tf_op jit(solution)/shard_map/pallas_call | solution.py:110
  41.3 0.0 copy-start.5
  41.3 1.3 copy-done.5
  42.7 40.4 %first_reduce.1 = bf16[2,2,2,8,128,128]{5,4,3,2,1,0:T(8,128)(2,1)S(1)} custom-call(f32[2,2,8,128,128]{4,3,2,1,0:T(8,128)} %bitcast.16, f32[2,2,8,128,128]{4,3,2,1,0:T(8,128)} %bitcast.17, bf16[2,2,8,128,128]{4,3,2,1,0:T(8,128)(2,1)S(1)} %bitcast.18, bf16[2,2,8,128,128]{4,3,2,1,0:T(8,128)(2,1)S(1)} %bitcast.19, f32[8,128]{1,0:T(8,128)S(1)} %constant_dynamic-slice_fusion.bias, ...), custom_call_target="tpu_custom_call" | custom-call | tf_op jit(solution)/shard_map/first_reduce/pallas_call | solution.py:244
  83.1 0.0 copy-start.6
  83.1 10.7 %shard_map.93 = (f32[64,128,128]{2,1,0:T(8,128)S(1)}, bf16[64,128,128]{2,1,0:T(8,128)(2,1)S(1)}) custom-call(s32[256]{0:T(256)S(1)} %reshape.38.cols_ref, s32[1]{0:T(128)} %bitcast.core_ref, bf16[2,32,128,128]{3,2,1,0:T(8,128)(2,1)S(1)} %bitcast.15, bf16[32,8,128,128]{3,2,1,0:T(8,128)(2,1)} %w_ref.5), custom_call_target="tpu_custom_call" | custom-call | flops 2147483648 | bytes 8388608 | tf_op jit(solution)/shard_map/pallas_call | solution.py:110
  93.8 0.0 copy-start.3
  93.8 1.9 %copy-done.3 = f32[64,128,128]{2,1,0:T(8,128)} copy-done((f32[64,128,128]{2,1,0:T(8,128)}, f32[64,128,128]{2,1,0:T(8,128)S(1)}, u32[]{:S(2)}) %copy-start.3) | copy-done | bytes 4194328
  95.8 0.0 copy-done.6
  95.8 51.9 %second_reduce.1 = bf16[128,2048]{1,0:T(8,128)(2,1)S(1)} custom-call(f32[64,128,128]{2,1,0:T(8,128)} %copy-done.3, bf16[64,128,128]{2,1,0:T(8,128)(2,1)S(1)} %get-tuple-element.16.away, f32[16,128]{1,0:T(8,128)S(1)} %bitcast.20), custom_call_target="tpu_custom_call" | custom-call | tf_op jit(solution)/shard_map/second_reduce/pallas_call | solution.py:364
  147.6 0.8 copy.19
  (2 shorter events, 0.0 us)
Async XLA Ops:
  0.0 8.6 %copy-start = (f32[8192]{0:T(1024)S(1)}, f32[8192]{0:T(1024)}, u32[]{:S(2)}) copy-start(f32[8192]{0:T(1024)} %param.13) | copy-start | bytes 98308
  0.0 2.7 %copy-start.7 = (bf16[128,8192]{1,0:T(8,128)(2,1)S(1)}, bf16[128,8192]{1,0:T(8,128)(2,1)}, u32[]{:S(2)}) copy-start(bf16[128,8192]{1,0:T(8,128)(2,1)} %param.9) | copy-start | bytes 6291460
  4.0 4.2 %copy-start.8 = (s32[128,64]{0,1:T(8,128)S(1)}, s32[128,64]{0,1:T(8,128)}, u32[]{:S(2)}) copy-start(s32[128,64]{0,1:T(8,128)} %param.14) | copy-start | bytes 98308
  4.0 4.4 %copy-start.9 = (s32[64,8]{0,1:T(8,128)S(1)}, s32[64,8]{0,1:T(8,128)}, u32[]{:S(2)}) copy-start(s32[64,8]{0,1:T(8,128)} %param.12) | copy-start | bytes 6148
  4.0 4.4 %copy-start.10 = (s32[64,8]{0,1:T(8,128)S(1)}, s32[64,8]{0,1:T(8,128)}, u32[]{:S(2)}) copy-start(s32[64,8]{0,1:T(8,128)} %param.16) | copy-start | bytes 6148
  5.2 27.9 %collective-permute-start = (bf16[128,4096]{1,0:T(8,128)(2,1)}, bf16[128,4096]{1,0:T(8,128)(2,1)S(1)}, u32[]{:S(2)}, u32[]{:S(2)}) collective-permute-start(bf16[128,4096]{1,0:T(8,128)(2,1)} %get-tuple-element.17), channel_id=1, source_target_pairs={{0,1},{1,0},{2,3},{3,2},{4,5},{5,4},{6,7},{7,6},{8,9},{9,8},{10,11... | collective-permute-start | bytes 3145736 | tf_op jit(solution)/shard_map/ppermute | solution.py:397
  8.3 24.7 %collective-permute-start.1 = (f32[128,64]{1,0:T(8,128)S(1)}, f32[128,64]{1,0:T(8,128)S(1)}, u32[]{:S(2)}, u32[]{:S(2)}) collective-permute-start(f32[128,64]{1,0:T(8,128)S(1)} %get-tuple-element.20), channel_id=1, source_target_pairs={{0,1},{1,0},{2,3},{3,2},{4,5},{5,4},{6,7},{7,6},{8,9},{9,8},{10,11... | collective-permute-start | bytes 98312 | tf_op jit(solution)/shard_map/ppermute | solution.py:408
  8.7 3.4 %copy-start.1 = (bf16[32,8,128,128]{3,2,1,0:T(8,128)(2,1)S(1)}, bf16[32,8,128,128]{3,2,1,0:T(8,128)(2,1)}, u32[]{:S(2)}) copy-start(bf16[32,8,128,128]{3,2,1,0:T(8,128)(2,1)} %w_ref.4) | copy-start | bytes 25165828
  17.0 1.3 copy-start.4
  33.0 3.4 %copy-start.2 = (bf16[32,8,128,128]{3,2,1,0:T(8,128)(2,1)S(1)}, bf16[32,8,128,128]{3,2,1,0:T(8,128)(2,1)}, u32[]{:S(2)}) copy-start(bf16[32,8,128,128]{3,2,1,0:T(8,128)(2,1)} %w_ref.4) | copy-start | bytes 25165828
  41.3 1.3 copy-start.5
  83.1 12.7 %copy-start.6 = (f32[2048]{0:T(1024)S(1)}, f32[2048]{0:T(1024)}, u32[]{:S(2)}) copy-start(f32[2048]{0:T(1024)} %param.17) | copy-start | bytes 24580
  93.8 2.0 %copy-start.3 = (f32[64,128,128]{2,1,0:T(8,128)}, f32[64,128,128]{2,1,0:T(8,128)S(1)}, u32[]{:S(2)}) copy-start(f32[64,128,128]{2,1,0:T(8,128)S(1)} %get-tuple-element.15.home) | copy-start | bytes 12582916
where the time goes:
time: 149 us; the launch traced here: 148 us
  Pallas kernels  113 us (76%)
  local copies, waits for them, and re-layouts  15.5 us (10%)
  waiting for transfers between devices  14.5 us (10%)
  starting transfers between devices  3.07 us (2%)
  other arithmetic  2.36 us (2%)
    pallas_call x1, Pallas kernels, second_reduce(): pl.pallas_call(functools.partial(second_reduce_kernel, n_col, parts), out...  51.9 us
    pallas_call x1, Pallas kernels, first_reduce(): pl.pallas_call(functools.partial(first_reduce_kernel, chunks), out_shape=...  40.4 us
    pallas_call x3, Pallas kernels, sparse_partial(): pl.pallas_call(functools.partial(sparse_kernel, per_step, entries, blocke...  20.6 us
    ppermute x1, waiting for transfers between devices, exchanged_rows(): lax.ppermute(mask2.astype(F32), 'depth', swap)  14.4 us
    unnamed x24, local copies, waits for them, and re-layouts  12.3 us
    ppermute x1, starting transfers between devices, exchanged_rows(): taken = lax.ppermute(give, 'depth', swap)  3 us
  transfers between devices with their start and end apart: 2, of which 1 were waited for; matrix products, arithmetic and copies ran while one was open for 0% of the time, Pallas kernels for 3%

commit v1 on v0

v1 whole, which is shorter than its diff:
```python
import functools

import jax
import jax.numpy as jnp
from jax import lax
from jax.experimental import pallas as pl
from jax.experimental.pallas import tpu as pltpu
from jax.sharding import PartitionSpec as P


def fold_function(inputs, targets, stride):

    def add_tiles(running_total, tiles, first_row):

        def advance(number, total):
            offset = number * stride
            block_list = lax.dynamic_slice_in_dim(tiles, offset, stride, 0)
            incoming_rows = lax.dynamic_slice_in_dim(inputs, offset, stride, 1)
            wanted = lax.dynamic_slice_in_dim(targets, offset, stride, 0)
            product = jnp.einsum(
                "tws,wish->twih", incoming_rows, block_list, preferred_element_type=jnp.float32
            )
            flat_product = product.reshape(product.shape[0], -1, product.shape[-1])
            return total.at[:, wanted.reshape(-1)].add(flat_product)

        return lax.fori_loop(0, tiles.shape[0] // stride, advance, running_total)

    return add_tiles


def gathered_weights(acts, act_mask, w1, cols1, bias1, mask2, w2, cols2, bias2):
    block = w1.shape[-1]
    rows_dev = acts.shape[0]
    row_blocks = act_mask.shape[1]
    col_blocks = mask2.shape[1]
    row_index = lax.axis_index("row")
    col_index = lax.axis_index("col")
    masked = acts.reshape(rows_dev, row_blocks, block) * act_mask[:, :, None].astype(jnp.bfloat16)
    first_layer_destinations = cols1 - col_index * col_blocks
    second_targets = cols2 - row_index * row_blocks
    first_offset_value = jnp.zeros((rows_dev, col_blocks, block), jnp.float32)
    first_fold = fold_function(masked, first_layer_destinations, w1.shape[0])
    first_sum = first_fold(
        first_offset_value, lax.all_gather(w1, "depth", axis=0, tiled=True), jnp.int32(0)
    )
    bias_blocks = bias1.reshape(col_blocks, block)
    share = col_blocks // lax.axis_size("row")
    part_sum = lax.psum_scatter(first_sum, "row", scatter_dimension=1, tiled=True)
    bias_part = lax.dynamic_slice_in_dim(bias_blocks, row_index * share, share, 0)
    mask_part = lax.dynamic_slice_in_dim(mask2, row_index * share, share, 1)
    hidden_part = jnp.maximum(part_sum + bias_part, 0.0) * mask_part[:, :, None].astype(jnp.float32)
    hidden = lax.all_gather(hidden_part.astype(jnp.bfloat16), "row", axis=1, tiled=True)
    second_start = jnp.zeros((rows_dev, row_blocks, block), jnp.float32)
    second_fold = fold_function(hidden, second_targets, w2.shape[0])
    second_sum = second_fold(
        second_start, lax.all_gather(w2, "depth", axis=0, tiled=True), jnp.int32(0)
    )
    outcome = lax.psum_scatter(second_sum, "col", scatter_dimension=1, tiled=True)
    bias_out = bias2.reshape(outcome.shape[1], block)
    return jnp.maximum(outcome + bias_out, 0.0).astype(jnp.bfloat16).reshape(rows_dev, -1)


MESH = pl.DeviceIdType.MESH
F32, BF16 = jnp.float32, jnp.bfloat16


def greet(partners):
    barrier = pltpu.get_barrier_semaphore()
    for partner in partners:
        pl.semaphore_signal(barrier, inc=1, device_id=partner, device_id_type=MESH)
    pl.semaphore_wait(barrier, len(partners))


def plan_rows(cols):
    stored, entries = cols.shape
    count = stored * entries
    small = cols.astype(BF16)

    def iota(shape, dim):
        return lax.broadcasted_iota(jnp.int32, shape, dim).astype(F32)

    def row_of(j):
        return jnp.floor((j + 0.5) * (1.0 / entries))

    lane = iota((entries, count), 1)
    spread = (lane - row_of(lane) * entries == iota((entries, count), 0)).astype(BF16)
    wide = jnp.dot(small, spread, preferred_element_type=F32)
    at = row_of(iota((stored, count), 1)) == iota((stored, count), 0)
    col_row = jnp.sum(jnp.where(at, wide, 0.0), axis=0, keepdims=True)
    down = (row_of(iota((count, stored), 0)) == iota((count, stored), 1)).astype(BF16)
    tall = jnp.dot(down, small, preferred_element_type=F32)
    line = iota((count, entries), 0)
    at = line - row_of(line) * entries == iota((count, entries), 1)
    col_col = jnp.sum(jnp.where(at, tall, 0.0), axis=1, keepdims=True)
    index_row, index_col = iota((1, count), 1), iota((count, 1), 0)
    key_row, key_col = col_row * count + index_row, col_col * count + index_col

    def total(flags, axis):
        return jnp.sum(jnp.where(flags, 1.0, 0.0), axis=axis, keepdims=True)

    rank = total(key_row < key_col, 1)
    less = total(col_row < col_col, 1)
    hit = rank == iota((count, count), 1)
    entry = jnp.sum(jnp.where(hit, index_col, 0.0), axis=0, keepdims=True)
    same = jnp.sum(jnp.where(hit, jnp.where(rank > less, 1.0, 0.0), 0.0), axis=0, keepdims=True)
    upto, below = total(col_col <= index_row, 0), total(col_col < index_row, 0)
    last = jnp.where(upto > below, upto - 1.0, float(count))
    return [row_of(entry), entry, same, last]


def prepare_kernel(acts, act_mask, cols1, cols2, mask2, staged, live_own, live_give, plan):
    r, c, d = lax.axis_index("row"), lax.axis_index("col"), lax.axis_index("depth")
    n_row = lax.axis_size("row")
    rows, row_blocks = act_mask.shape
    col_blocks = mask2.shape[1]
    block = staged.shape[-1]
    stored, size = row_blocks // 2, rows // 2
    mask = act_mask[...].astype(F32).astype(BF16)
    for b in range(row_blocks):
        where = (b // stored + d) % 2
        value = acts[:, b * block:(b + 1) * block] * mask[:, b:b + 1]
        for rc in range(2):
            staged[where, rc, b % stored] = value[rc * size:(rc + 1) * size]
    live = mask2[...].astype(F32).astype(BF16)
    share = col_blocks // 2 // n_row
    source = lax.broadcasted_iota(jnp.int32, (col_blocks, live_own.shape[1]), 0)
    target = lax.broadcasted_iota(jnp.int32, (col_blocks, live_own.shape[1]), 1)
    for ref, half in ((live_own, d), (live_give, 1 - d)):
        pick = (source == target + (half * (col_blocks // 2) + r * share)) & (target < share)
        pick = jnp.where(pick, 1.0, 0.0).astype(BF16)
        ref[...] = jnp.dot(live, pick, preferred_element_type=F32).astype(BF16)
    held = cols1.shape[0] // 2
    at = pl.ds(pl.multiple_of(d * held, 8), held)
    local1 = (cols1[at, :] - c * col_blocks).astype(F32)
    local2 = (cols2[at, :] - r * row_blocks).astype(F32)
    for n, value in enumerate(plan_rows(local1) + plan_rows(local2)):
        plan[n:n + 1, :] = value.astype(jnp.int32)


def prepare(acts, act_mask, cols1, cols2, mask2, block):
    rows, row_blocks = act_mask.shape
    count = cols1.shape[0] // 2 * cols1.shape[1]
    vmem = pl.BlockSpec(memory_space=pltpu.VMEM)
    return pl.pallas_call(
        prepare_kernel,
        out_shape=[
            jax.ShapeDtypeStruct((2, 2, row_blocks // 2, rows // 2, block), BF16),
            jax.ShapeDtypeStruct((rows, 128), BF16),
            jax.ShapeDtypeStruct((rows, 128), BF16),
            jax.ShapeDtypeStruct((8, count), jnp.int32),
        ],
        in_specs=[vmem] * 5,
        out_specs=[vmem] * 4,
        name="prepare",
    )(acts, act_mask, cols1, cols2, mask2)


def each(count, body, width=2):
    def step(at, carry):
        for u in range(width):
            body(at * width + u)
        return carry

    lax.fori_loop(0, count // width, step, 0)


def layers_kernel(
    n_col, plan, staged, live_own, live_give, bias1, bias2, w1, w2, out,
    wbuf, sums, acts_in0, acts_in1, live_in, kept, given, core_in, y_out, y_in, x_out, x_in,
    x1_00, x1_01, x1_10, x1_11, away, home, y2_in, z_out, z_in,
    load_sem, acts_send, acts_recv, live_sem, send_sem, recv_sem,
    send_y, recv_y, send_z, recv_z,
):
    r, c, d = lax.axis_index("row"), lax.axis_index("col"), lax.axis_index("depth")
    x, core = r // 2, r % 2
    partner = {"row": x * 2 + 1 - core}
    y_peer = {"depth": 1 - d}
    x_peer = {"row": (1 - x) * 2 + core}
    near = c % 2
    z_mate = {"col": c + 1 - 2 * near}
    entries, block = wbuf.shape[0], wbuf.shape[-1]
    size = sums.shape[1]
    share1 = bias1.shape[0]
    share2 = bias2.shape[0]
    acts_in = (acts_in0, acts_in1)
    x1 = ((x1_00, x1_01), (x1_10, x1_11))
    started = []

    def remote(source, target, send, recv, device):
        return pltpu.make_async_remote_copy(
            src_ref=source, dst_ref=target, send_sem=send, recv_sem=recv,
            device_id=device, device_id_type=MESH,
        )

    def begin(copy):
        copy.start()
        started.append(copy)

    def load(source, which):
        return pltpu.make_async_copy(source, wbuf, load_sem.at[which])

    load(w1, 0).start()
    greet([partner, y_peer, x_peer] + [{"col": lax.rem(c + o, n_col)} for o in range(1, n_col)])

    piece_blocks = acts_in0.shape[0] // 4

    def piece(which, part):
        return pl.ds((which * 2 + part) * piece_blocks, piece_blocks)

    for rc in range(2):
        for part in range(2):
            begin(remote(
                staged.at[1, rc, piece(near, part)], acts_in[rc].at[piece(near, part)],
                acts_send.at[0, rc, part], acts_recv.at[0, rc, part], y_peer,
            ))
    begin(remote(live_give, live_in, live_sem.at[0], live_sem.at[1], y_peer))

    def arrived(target, send, recv):
        remote(target, target, send, recv, y_peer).wait_recv()

    def pass_on(rc, part):
        mine = acts_in[rc].at[piece(near, part)]
        arrived(mine, acts_send.at[0, rc, part], acts_recv.at[0, rc, part])
        begin(remote(mine, mine, acts_send.at[1, rc, part], acts_recv.at[1, rc, part], z_mate))

    def passed(rc):
        for part in range(2):
            theirs = acts_in[rc].at[piece(1 - near, part)]
            arrived(theirs, acts_send.at[1, rc, part], acts_recv.at[1, rc, part])

    sums[entries] = jnp.zeros(sums.shape[1:], F32)

    def multiply(x_ref, layer):
        width = 16 if entries % 16 == 0 else 1

        def step(at, running):
            for u in range(width):
                p = at * width + u
                product = jnp.dot(
                    x_ref[plan[layer * 4, p]], wbuf[plan[layer * 4 + 1, p]],
                    preferred_element_type=F32,
                )
                running = running * plan[layer * 4 + 2, p].astype(F32) + product
                sums[p] = running
            return running

        lax.fori_loop(0, entries // width, step, jnp.zeros(sums.shape[1:], F32))

    def column(layer, b):
        return sums[plan[layer * 4 + 3, b]]

    def first_partial(h, rc):
        multiply(acts_in[rc] if h else staged.at[0, rc], 0)

        def split(q):
            at = (q // share1) * 2 * share1 + q % share1
            kept[h, rc, q] = column(0, at + core * share1)
            given[h, rc, q] = column(0, at + (1 - core) * share1).astype(BF16)

        each(kept.shape[2], split)
        send(0, given.at[h, rc], core_in.at[h, rc], h, rc, h, partner)

    def send(stage, source, target, h, rc, landing, device):
        begin(remote(
            source, target, send_sem.at[stage, h, rc], recv_sem.at[stage, landing, rc], device
        ))

    def await_stage(stage, target, h, rc):
        arrived(target, send_sem.at[stage, h, rc], recv_sem.at[stage, h, rc])

    half = kept.shape[2] // 2
    quarter = half // 2

    def pair(h, rc):
        await_stage(0, core_in.at[h, rc], h, rc)

        def other(q):
            at = (1 - d) * half + q
            y_out[h, rc, q] = (kept[h, rc, at] + core_in[h, rc, at].astype(F32)).astype(BF16)

        def own(q):
            at = d * half + q
            kept[h, rc, at] = kept[h, rc, at] + core_in[h, rc, at].astype(F32)

        each(half, other)
        send(1, y_out.at[h, rc], y_in.at[1 - h, rc], h, rc, 1 - h, y_peer)
        each(half, own)

    def along_y(h, rc):
        await_stage(1, y_in.at[h, rc], h, rc)

        def body(q):
            at = (1 - x) * quarter + q
            x_out[h, rc, q] = (
                kept[h, rc, d * half + at] + y_in[h, rc, at].astype(F32)
            ).astype(BF16)

        each(quarter, body)
        send(2, x_out.at[h, rc], x_in.at[h, rc], h, rc, h, x_peer)

    def slot(h, rc, row):
        return x1[h][rc].at[pl.ds(row * share1, share1)]

    def along_x(h, rc):
        await_stage(2, x_in.at[h, rc], h, rc)
        live = (live_in if h else live_own)[rc * size:(rc + 1) * size, :].astype(F32)
        for b in range(share1):
            at = x * quarter + b
            z = (
                kept[h, rc, d * half + at] + y_in[h, rc, at].astype(F32)
                + x_in[h, rc, b].astype(F32)
            )
            value = jnp.maximum(z + bias1[b:b + 1, :], 0.0) * live[:, b:b + 1]
            x1[h][rc][r * share1 + b] = value.astype(BF16)
        mine = slot(h, rc, r)
        send(3, mine, mine, h, rc, h, x_peer)
        send(4, mine, mine, h, rc, h, partner)

    def forward(h, rc):
        theirs = slot(h, rc, (1 - x) * 2 + core)
        await_stage(3, theirs, h, rc)
        send(5, theirs, theirs, h, rc, h, partner)

    def second_partial(h, rc):
        await_stage(4, slot(h, rc, x * 2 + 1 - core), h, rc)
        await_stage(5, slot(h, rc, (1 - x) * 2 + 1 - core), h, rc)
        multiply(x1[h][rc], 1)

        def body(b):
            if h:
                away[rc, b] = column(1, b).astype(BF16)
            else:
                home[rc, b] = column(1, b)

        each(home.shape[1], body)

    last = n_col - 1
    upper = c // 2
    inner = c + upper * (last - 2 * c)

    def mirrored(value):
        return value + upper * (last - 2 * value)

    def owner(i):
        end, mid = (3, 2, 1, 0)[i], (2, 0, 3, 1)[i]
        return mirrored(end + inner * (mid - end))

    def receiver(i):
        end, mid = (1, 2, 1)[i], (2, 0, 3)[i]
        return mirrored(end + inner * (mid - end))

    def y_copy(i, p):
        return remote(
            away.at[p, pl.ds(owner(i) * share2, share2)], y2_in.at[i, p],
            send_y.at[i, p], recv_y.at[i, p], y_peer,
        )

    def z_copy(i, p):
        at = 3 * inner if i == 0 else i
        return remote(
            z_out.at[i, p], z_in.at[at, p], send_z.at[i, p], recv_z.at[at, p],
            {"col": receiver(i)},
        )

    def z_arrival(at, p):
        remote(
            z_in.at[at, p], z_in.at[at, p], send_z.at[0, p], recv_z.at[at, p],
            {"col": receiver(0)},
        ).wait_recv()

    def near_sum(i, p, b):
        return home[p, owner(i) * share2 + b] + y2_in[i, p, b].astype(F32)

    def along_z(i, p):
        y_copy(i, p).wait_recv()

        def plain(b):
            z_out[i, p, b] = near_sum(i, p, b).astype(BF16)

        def joined(b):
            z_out[i, p, b] = (near_sum(i, p, b) + z_in[0, p, b].astype(F32)).astype(BF16)

        if i == 2:
            @pl.when(inner == 1)
            def _():
                z_arrival(0, p)
                each(share2, joined)

            @pl.when(inner == 0)
            def _():
                each(share2, plain)
        else:
            each(share2, plain)
        z_copy(i, p).start()

    def finish(p, slots):
        for at in slots:
            z_arrival(at, p)
        for b in range(share2):
            value = home[p, c * share2 + b] + y2_in[last, p, b].astype(F32)
            for at in slots:
                value += z_in[at, p, b].astype(F32)
            value = jnp.maximum(value + bias2[b:b + 1, :], 0.0)
            out[p * size:(p + 1) * size, b * block:(b + 1) * block] = value.astype(BF16)

    load(w1, 0).wait()
    first_partial(0, 0)
    pass_on(0, 0)
    first_partial(0, 1)
    pass_on(0, 1)
    pair(0, 0)
    pair(0, 1)
    pass_on(1, 0)
    pass_on(1, 1)
    passed(0)
    first_partial(1, 0)
    pair(1, 0)
    passed(1)
    first_partial(1, 1)
    load(w2, 1).start()
    arrived(live_in, live_sem.at[0], live_sem.at[1])
    along_y(1, 0)
    pair(1, 1)
    along_y(1, 1)
    along_x(1, 0)
    along_x(1, 1)
    forward(1, 0)
    along_y(0, 0)
    load(w2, 1).wait()
    second_partial(1, 0)
    y_copy(0, 0).start()
    forward(1, 1)
    along_x(0, 0)
    second_partial(1, 1)
    y_copy(0, 1).start()
    for i in range(1, n_col):
        for p in range(2):
            y_copy(i, p).start()
    along_y(0, 1)
    forward(0, 0)
    second_partial(0, 0)
    along_x(0, 1)
    along_z(0, 0)
    forward(0, 1)
    second_partial(0, 1)
    along_z(0, 1)
    for i in range(1, last):
        for p in range(2):
            along_z(i, p)
    for p in range(2):
        y_copy(last, p).wait_recv()

        @pl.when(inner == 1)
        def _():
            finish(p, (1, 2, 3))

        @pl.when(inner == 0)
        def _():
            finish(p, (1, 2))
    for copy in started:
        copy.wait_send()
    for i in range(n_col):
        for p in range(2):
            y_copy(i, p).wait_send()
            if i < last:
                z_copy(i, p).wait_send()


def fused_layers(acts, act_mask, w1, cols1, bias1, mask2, w2, cols2, bias2):
    block = w1.shape[-1]
    stored = w1.shape[0]
    rows = acts.shape[0]
    row_blocks, col_blocks = act_mask.shape[1], mask2.shape[1]
    n_row, n_col = lax.axis_size("row"), lax.axis_size("col")
    r, d = lax.axis_index("row"), lax.axis_index("depth")
    size = rows // 2
    share1 = col_blocks // 2 // n_row
    share2 = row_blocks // n_col
    staged, live_own, live_give, plan = prepare(acts, act_mask, cols1, cols2, mask2, block)
    first = d * (col_blocks // 2) + r * share1
    bias_part = lax.dynamic_slice_in_dim(bias1.reshape(col_blocks, block), first, share1, 0)
    flat1, flat2 = w1.reshape(-1, block, block), w2.reshape(-1, block, block)
    count = flat1.shape[0]
    half = col_blocks // 2
    smem = pl.BlockSpec(memory_space=pltpu.SMEM)
    vmem = pl.BlockSpec(memory_space=pltpu.VMEM)
    hbm = pl.BlockSpec(memory_space=pl.ANY)
    tile = (size, block)
    dma = pltpu.SemaphoreType.DMA
    return pl.pallas_call(
        functools.partial(layers_kernel, n_col),
        out_shape=jax.ShapeDtypeStruct((rows, share2 * block), BF16),
        in_specs=[smem] + [vmem] * 5 + [hbm] * 2,
        out_specs=vmem,
        scratch_shapes=[
            pltpu.VMEM((count, block, block), BF16),
            pltpu.VMEM((count + 1, *tile), F32),
            pltpu.VMEM((stored, *tile), BF16),
            pltpu.VMEM((stored, *tile), BF16),
            pltpu.VMEM((rows, 128), BF16),
            pltpu.VMEM((2, 2, half, *tile), F32),
            pltpu.VMEM((2, 2, half, *tile), BF16),
            pltpu.VMEM((2, 2, half, *tile), BF16),
            pltpu.VMEM((2, 2, half // 2, *tile), BF16),
            pltpu.VMEM((2, 2, half // 2, *tile), BF16),
            pltpu.VMEM((2, 2, share1, *tile), BF16),
            pltpu.VMEM((2, 2, share1, *tile), BF16),
            pltpu.VMEM((half, *tile), BF16),
            pltpu.VMEM((half, *tile), BF16),
            pltpu.VMEM((half, *tile), BF16),
            pltpu.VMEM((half, *tile), BF16),
            pltpu.VMEM((2, row_blocks, *tile), BF16),
            pltpu.VMEM((2, row_blocks, *tile), F32),
            pltpu.VMEM((n_col, 2, share2, *tile), BF16),
            pltpu.VMEM((n_col - 1, 2, share2, *tile), BF16),
            pltpu.VMEM((n_col, 2, share2, *tile), BF16),
            dma((2,)),
            dma((2, 2, 2)),
            dma((2, 2, 2)),
            dma((2,)),
            dma((6, 2, 2)),
            dma((6, 2, 2)),
            dma((n_col, 2)),
            dma((n_col, 2)),
            dma((n_col - 1, 2)),
            dma((n_col, 2)),
        ],
        compiler_params=pltpu.CompilerParams(
            collective_id=1, has_side_effects=True, vmem_limit_bytes=60 * 1024 * 1024
        ),
        name="layers",
    )(plan, staged, live_own, live_give, bias_part, bias2.reshape(share2, block), flat1, flat2)


def solution(mesh):
    near = mesh.shape["depth"] == 2 and mesh.shape["row"] == 4 and mesh.shape["col"] == 4
    return jax.shard_map(
        fused_layers if near else gathered_weights,
        mesh=mesh,
        in_specs=(
            P("depth", "row"),
            P("depth", "row"),
            P(("row", "depth"), "col", None, None),
            P("row", "col"),
            P("col"),
            P("depth", "col"),
            P(("col", "depth"), "row", None, None),
            P("col", "row"),
            P(("row", "col")),
        ),
        out_specs=P("depth", ("row", "col")),
        check_vma=False,
    )
```

time: 149 us -> 118 us (0.79)
  waiting for transfers between devices: 14.5 us -> 0 us
  local copies, waits for them, and re-layouts: 15.5 us -> 8.93 us
  Pallas kernels: 113 us -> 108 us
  starting transfers between devices: 3.07 us -> 0 us
  other arithmetic: 2.36 us -> 0 us
    ppermute x2 -> x0, waiting for transfers between devices: 14.5 us -> none  [the longest x1 14.4 us: exchanged_rows(): lax.ppermute(mask2.astype(F32), 'depth', swap)]
    pallas_call x5 -> x2, Pallas kernels: 113 us -> 108 us  [the longest x1 105 us: fused_layers(): pl.pallas_call(functools.partial(layers_kernel, n_col), out_shape=jax.Sha...]
    unnamed x24 -> x7, local copies, waits for them, and re-layouts: 12.3 us -> 8.34 us
    ppermute x2 -> x0, starting transfers between devices: 3.07 us -> none  [the longest x1 3 us: exchanged_rows(): taken = lax.ppermute(give, 'depth', swap)]
    mul x1 -> x0, local copies, waits for them, and re-layouts: 1.63 us -> none  [exchanged_rows(): acts.reshape(rows, row_blocks, block) * act_mask[:, :, None].astype(BF16)]
  transfers between devices with their start and end apart: 2 -> 0, of which waited for: 1 -> 0; matrix products, arithmetic and copies ran while one was open for 0% -> 0% of each run, Pallas kernels for 3% -> 0%
where the time goes in v1:
time: 118 us; the launch traced here: 117 us
  Pallas kernels  108 us (92%)
  local copies, waits for them, and re-layouts  8.93 us (8%)
    pallas_call x1, Pallas kernels, fused_layers(): pl.pallas_call(functools.partial(layers_kernel, n_col), out_shape=jax.Sha...  105 us
    unnamed x7, local copies, waits for them, and re-layouts  8.34 us
    pallas_call x1, Pallas kernels, prepare(): pl.pallas_call(prepare_kernel, out_shape=[jax.ShapeDtypeStruct((2, 2, row...  3.76 us

profile of v1, /device:TPU:0, one launch (start us, length us, event | category | flops | bytes accessed | tf_op | source)
XLA Modules:
  0.0 117.3 jit_solution(6821489224110529925)
XLA Ops:
  0.0 0.0 copy-start
  0.0 0.8 copy-done
  0.8 0.6 constant_dynamic-slice_fusion.bias1
  1.3 1.4 %copy.11.cols1 = s32[64,8]{1,0:T(8,128)} copy(s32[64,8]{0,1:T(8,128)} %param.12) | data formatting | bytes 4096 | tf_op args[3]
  2.7 1.4 %copy.12.cols2 = s32[64,8]{1,0:T(8,128)} copy(s32[64,8]{0,1:T(8,128)} %param.16) | data formatting | bytes 4096 | tf_op args[7]
  4.1 1.5 %copy.10.act_mask = s32[128,64]{1,0:T(8,128)} copy(s32[128,64]{0,1:T(8,128)} %param.10) | data formatting | bytes 65536 | tf_op args[1]
  5.6 1.5 %copy.13.mask2 = s32[128,64]{1,0:T(8,128)} copy(s32[128,64]{0,1:T(8,128)} %param.14) | data formatting | bytes 65536 | tf_op args[5]
  7.1 3.8 %prepare.1 = (bf16[2,2,32,64,128]{4,3,2,1,0:T(8,128)(2,1)}, bf16[128,128]{1,0:T(8,128)(2,1)}, bf16[128,128]{1,0:T(8,128)(2,1)}, s32[8,256]{1,0:T(8,128)}) custom-call(bf16[128,8192]{1,0:T(8,128)(2,1)} %acts.1, s32[128,64]{1,0:T(8,128)} %copy.10.act_mask, s32[64,8]{1,0:T(8,128)} %copy.11.cols1, s32[64,8]{1,0:T(8,128)} %copy.12.cols2, s32[128,64]{1,0:T(8,128)} %copy.13.mask2), custom_call_target="tpu_custom_call" | custom-call | tf_op jit(solution)/shard_map/prepare/pallas_call | solution.py:144
  10.8 104.6 %layers.1 = bf16[128,2048]{1,0:T(8,128)(2,1)} custom-call(s32[8,256]{1,0:T(8,128)} %get-tuple-element.9.plan, bf16[2,2,32,64,128]{4,3,2,1,0:T(8,128)(2,1)} %get-tuple-element.10.staged, bf16[128,128]{1,0:T(8,128)(2,1)} %get-tuple-element.11.live_own, bf16[128,128]{1,0:T(8,128)(2,1)} %get-tuple-element.12.live_give, ...), custom_call_target="tpu_custom_call" | custom-call | tf_op jit(solution)/shard_map/layers/pallas_call | solution.py:490
  115.4 1.9 %copy.15 = bf16[128,2048]{1,0:T(8,128)(2,1)} copy(bf16[128,2048]{1,0:T(8,128)(2,1)} %layers.1) | data formatting | bytes 1048576
Async XLA Ops:
  0.0 0.8 copy-start

commit v2 on v1

--- a/solution.py
+++ b/solution.py
@@ -64,15 +64,8 @@
 F32, BF16 = jnp.float32, jnp.bfloat16
 
 
-def greet(partners):
-    barrier = pltpu.get_barrier_semaphore()
-    for partner in partners:
-        pl.semaphore_signal(barrier, inc=1, device_id=partner, device_id_type=MESH)
-    pl.semaphore_wait(barrier, len(partners))
-
-
-def plan_rows(cols):
-    stored, entries = cols.shape
+def plan_rows(cols, first, stored):
+    entries = cols.shape[0]
     count = stored * entries
     small = cols.astype(BF16)
 
@@ -82,13 +75,17 @@
     def row_of(j):
         return jnp.floor((j + 0.5) * (1.0 / entries))
 
+    tall_shape = (cols.shape[1], count)
+    spread = row_of(iota(tall_shape, 1)) + first.astype(F32) == iota(tall_shape, 0)
+    spread = jnp.where(spread, 1.0, 0.0).astype(BF16)
+    wide = jnp.dot(small, spread, preferred_element_type=F32)
     lane = iota((entries, count), 1)
-    spread = (lane - row_of(lane) * entries == iota((entries, count), 0)).astype(BF16)
-    wide = jnp.dot(small, spread, preferred_element_type=F32)
-    at = row_of(iota((stored, count), 1)) == iota((stored, count), 0)
+    at = lane - row_of(lane) * entries == iota((entries, count), 0)
     col_row = jnp.sum(jnp.where(at, wide, 0.0), axis=0, keepdims=True)
-    down = (row_of(iota((count, stored), 0)) == iota((count, stored), 1)).astype(BF16)
-    tall = jnp.dot(down, small, preferred_element_type=F32)
+    down_shape = (count, cols.shape[1])
+    down = row_of(iota(down_shape, 0)) + first.astype(F32) == iota(down_shape, 1)
+    down = jnp.where(down, 1.0, 0.0).astype(BF16)
+    tall = lax.dot_general(down, small, (((1,), (1,)), ((), ())), preferred_element_type=F32)
     line = iota((count, entries), 0)
     at = line - row_of(line) * entries == iota((count, entries), 1)
     col_col = jnp.sum(jnp.where(at, tall, 0.0), axis=1, keepdims=True)
@@ -108,53 +105,6 @@
     return [row_of(entry), entry, same, last]
 
 
-def prepare_kernel(acts, act_mask, cols1, cols2, mask2, staged, live_own, live_give, plan):
-    r, c, d = lax.axis_index("row"), lax.axis_index("col"), lax.axis_index("depth")
-    n_row = lax.axis_size("row")
-    rows, row_blocks = act_mask.shape
-    col_blocks = mask2.shape[1]
-    block = staged.shape[-1]
-    stored, size = row_blocks // 2, rows // 2
-    mask = act_mask[...].astype(F32).astype(BF16)
-    for b in range(row_blocks):
-        where = (b // stored + d) % 2
-        value = acts[:, b * block:(b + 1) * block] * mask[:, b:b + 1]
-        for rc in range(2):
-            staged[where, rc, b % stored] = value[rc * size:(rc + 1) * size]
-    live = mask2[...].astype(F32).astype(BF16)
-    share = col_blocks // 2 // n_row
-    source = lax.broadcasted_iota(jnp.int32, (col_blocks, live_own.shape[1]), 0)
-    target = lax.broadcasted_iota(jnp.int32, (col_blocks, live_own.shape[1]), 1)
-    for ref, half in ((live_own, d), (live_give, 1 - d)):
-        pick = (source == target + (half * (col_blocks // 2) + r * share)) & (target < share)
-        pick = jnp.where(pick, 1.0, 0.0).astype(BF16)
-        ref[...] = jnp.dot(live, pick, preferred_element_type=F32).astype(BF16)
-    held = cols1.shape[0] // 2
-    at = pl.ds(pl.multiple_of(d * held, 8), held)
-    local1 = (cols1[at, :] - c * col_blocks).astype(F32)
-    local2 = (cols2[at, :] - r * row_blocks).astype(F32)
-    for n, value in enumerate(plan_rows(local1) + plan_rows(local2)):
-        plan[n:n + 1, :] = value.astype(jnp.int32)
-
-
-def prepare(acts, act_mask, cols1, cols2, mask2, block):
-    rows, row_blocks = act_mask.shape
-    count = cols1.shape[0] // 2 * cols1.shape[1]
-    vmem = pl.BlockSpec(memory_space=pltpu.VMEM)
-    return pl.pallas_call(
-        prepare_kernel,
-        out_shape=[
-            jax.ShapeDtypeStruct((2, 2, row_blocks // 2, rows // 2, block), BF16),
-            jax.ShapeDtypeStruct((rows, 128), BF16),
-            jax.ShapeDtypeStruct((rows, 128), BF16),
-            jax.ShapeDtypeStruct((8, count), jnp.int32),
-        ],
-        in_specs=[vmem] * 5,
-        out_specs=[vmem] * 4,
-        name="prepare",
-    )(acts, act_mask, cols1, cols2, mask2)
-
-
 def each(count, body, width=2):
     def step(at, carry):
         for u in range(width):
@@ -165,13 +115,17 @@
 
 
 def layers_kernel(
-    n_col, plan, staged, live_own, live_give, bias1, bias2, w1, w2, out,
-    wbuf, sums, acts_in0, acts_in1, live_in, kept, given, core_in, y_out, y_in, x_out, x_in,
+    n_col, fronts, acts, act_mask, cols1, cols2, mask2, bias1, bias2, w1, w2, out,
+    wbuf, wbuf2, sums, acts_in0, acts_in1, keep_raw, give_raw, keep, give,
+    act_mask_v, cols1_v, cols2_v, mask2_v, bias1_v, bias2_v, plan_v, plan, live_in,
+    kept, given, core_in, y_out, y_in, x_out, x_in,
     x1_00, x1_01, x1_10, x1_11, away, home, y2_in, z_out, z_in,
+    front, front_out, front_in, front_y_out, front_y_in,
     load_sem, acts_send, acts_recv, live_sem, send_sem, recv_sem,
-    send_y, recv_y, send_z, recv_z,
+    send_y, recv_y, send_z, recv_z, send_f, recv_f, send_fy, recv_fy,
 ):
     r, c, d = lax.axis_index("row"), lax.axis_index("col"), lax.axis_index("depth")
+    n_row = lax.axis_size("row")
     x, core = r // 2, r % 2
     partner = {"row": x * 2 + 1 - core}
     y_peer = {"depth": 1 - d}
@@ -180,11 +134,49 @@
     z_mate = {"col": c + 1 - 2 * near}
     entries, block = wbuf.shape[0], wbuf.shape[-1]
     size = sums.shape[1]
-    share1 = bias1.shape[0]
+    stored = acts_in0.shape[0]
+    share1 = x_in.shape[2]
     share2 = bias2.shape[0]
     acts_in = (acts_in0, acts_in1)
     x1 = ((x1_00, x1_01), (x1_10, x1_11))
     started = []
+
+    loads = []
+
+    def load(source, target):
+        copy = pltpu.make_async_copy(source, target, load_sem.at[len(loads)])
+        copy.start()
+        loads.append(copy)
+        return copy
+
+    half_blocks = stored // 2
+    give_first = pl.multiple_of((1 - d) * stored + near * half_blocks, half_blocks)
+    keep_first = pl.multiple_of(d * stored, stored)
+    mask_loads = [load(act_mask, act_mask_v)]
+    give_loads = [
+        load(
+            acts.at[pl.ds(rc * size, size), pl.ds(give_first * block, half_blocks * block)],
+            give_raw.at[rc],
+        )
+        for rc in range(2)
+    ]
+    plan_loads = [load(cols1, cols1_v), load(cols2, cols2_v)]
+    keep_loads = [
+        load(
+            acts.at[pl.ds(rc * size, size), pl.ds(keep_first * block, stored * block)],
+            keep_raw.at[rc],
+        )
+        for rc in range(2)
+    ]
+    small_loads = [load(mask2, mask2_v), load(bias1, bias1_v), load(bias2, bias2_v)]
+    w1_load = load(w1, wbuf)
+    w2_load = load(w2, wbuf2)
+
+    barrier = pltpu.get_barrier_semaphore()
+    greeted = [partner, y_peer, x_peer]
+    greeted += [{"col": lax.rem(c + o, n_col)} for o in range(1, n_col)]
+    for device in greeted:
+        pl.semaphore_signal(barrier, inc=1, device_id=device, device_id_type=MESH)
 
     def remote(source, target, send, recv, device):
         return pltpu.make_async_remote_copy(
@@ -196,24 +188,63 @@
         copy.start()
         started.append(copy)
 
-    def load(source, which):
-        return pltpu.make_async_copy(source, wbuf, load_sem.at[which])
-
-    load(w1, 0).start()
-    greet([partner, y_peer, x_peer] + [{"col": lax.rem(c + o, n_col)} for o in range(1, n_col)])
-
-    piece_blocks = acts_in0.shape[0] // 4
+    parts = acts_send.shape[2]
+    piece_blocks = half_blocks // parts
 
     def piece(which, part):
-        return pl.ds((which * 2 + part) * piece_blocks, piece_blocks)
-
+        return pl.ds(which * half_blocks + part * piece_blocks, piece_blocks)
+
+    def mask_blocks(first, count):
+        rows = act_mask_v[pl.ds(first, count), :]
+        return rows.astype(F32).T.astype(BF16)
+
+    def hand_over(rc, part):
+        begin(remote(
+            give.at[rc, pl.ds(part * piece_blocks, piece_blocks)],
+            acts_in[rc].at[piece(near, part)],
+            acts_send.at[0, rc, part], acts_recv.at[0, rc, part], y_peer,
+        ))
+
+    for copy in mask_loads:
+        copy.wait()
+    give_mask = mask_blocks(give_first, half_blocks)
     for rc in range(2):
-        for part in range(2):
-            begin(remote(
-                staged.at[1, rc, piece(near, part)], acts_in[rc].at[piece(near, part)],
-                acts_send.at[0, rc, part], acts_recv.at[0, rc, part], y_peer,
-            ))
-    begin(remote(live_give, live_in, live_sem.at[0], live_sem.at[1], y_peer))
+        give_loads[rc].wait()
+        for b in range(half_blocks):
+            give[rc, b] = (
+                give_raw[rc, :, b * block:(b + 1) * block]
+                * give_mask[rc * size:(rc + 1) * size, b:b + 1]
+            )
+        if rc == 0:
+            pl.semaphore_wait(barrier, len(greeted))
+        for part in range(1 if rc else parts):
+            hand_over(rc, part)
+    for copy in plan_loads:
+        copy.wait()
+    held = cols1.shape[1] // 2
+    local1 = plan_rows((cols1_v[...] - c * n_row * 2 * share1).astype(F32), d * held, held)
+    local2 = plan_rows((cols2_v[...] - r * n_col * share2).astype(F32), d * held, held)
+    for n, value in enumerate(local1 + local2):
+        top = (stored - 1, entries - 1, 1, entries)[n % 4]
+        plan_v[n:n + 1, :] = jnp.clip(value.astype(jnp.int32), 0, top)
+    plan_copy = load(plan_v, plan)
+    keep_mask = mask_blocks(keep_first, stored)
+    for rc in range(2):
+        keep_loads[rc].wait()
+        for b in range(stored):
+            keep[rc, b] = (
+                keep_raw[rc, :, b * block:(b + 1) * block]
+                * keep_mask[rc * size:(rc + 1) * size, b:b + 1]
+            )
+    for copy in small_loads:
+        copy.wait()
+    share_rows = n_row * share1
+
+    def live_rows(side):
+        return mask2_v.at[pl.ds(pl.multiple_of(side * share_rows + r * share1, share1), share1)]
+
+    begin(remote(live_rows(1 - d), live_in, live_sem.at[0], live_sem.at[1], y_peer))
+    plan_copy.wait()
 
     def arrived(target, send, recv):
         remote(target, target, send, recv, y_peer).wait_recv()
@@ -224,20 +255,21 @@
         begin(remote(mine, mine, acts_send.at[1, rc, part], acts_recv.at[1, rc, part], z_mate))
 
     def passed(rc):
-        for part in range(2):
+        for part in range(parts):
             theirs = acts_in[rc].at[piece(1 - near, part)]
             arrived(theirs, acts_send.at[1, rc, part], acts_recv.at[1, rc, part])
 
     sums[entries] = jnp.zeros(sums.shape[1:], F32)
 
     def multiply(x_ref, layer):
-        width = 16 if entries % 16 == 0 else 1
+        weights = wbuf2 if layer else wbuf
+        width = 64 if entries % 64 == 0 else 1
 
         def step(at, running):
             for u in range(width):
                 p = at * width + u
                 product = jnp.dot(
-                    x_ref[plan[layer * 4, p]], wbuf[plan[layer * 4 + 1, p]],
+                    x_ref[plan[layer * 4, p]], weights[plan[layer * 4 + 1, p]],
                     preferred_element_type=F32,
                 )
                 running = running * plan[layer * 4 + 2, p].astype(F32) + product
@@ -250,7 +282,7 @@
         return sums[plan[layer * 4 + 3, b]]
 
     def first_partial(h, rc):
-        multiply(acts_in[rc] if h else staged.at[0, rc], 0)
+        multiply(acts_in[rc] if h else keep.at[rc], 0)
 
         def split(q):
             at = (q // share1) * 2 * share1 + q % share1
@@ -303,14 +335,15 @@
 
     def along_x(h, rc):
         await_stage(2, x_in.at[h, rc], h, rc)
-        live = (live_in if h else live_own)[rc * size:(rc + 1) * size, :].astype(F32)
+        live = (live_in if h else live_rows(d))[...].astype(F32).T[rc * size:(rc + 1) * size]
+        shift = bias1_v[pl.ds(pl.multiple_of((d * n_row + r) * share1, share1), share1), :]
         for b in range(share1):
             at = x * quarter + b
             z = (
                 kept[h, rc, d * half + at] + y_in[h, rc, at].astype(F32)
                 + x_in[h, rc, b].astype(F32)
             )
-            value = jnp.maximum(z + bias1[b:b + 1, :], 0.0) * live[:, b:b + 1]
+            value = jnp.maximum(z + shift[b:b + 1, :], 0.0) * live[:, b:b + 1]
             x1[h][rc][r * share1 + b] = value.astype(BF16)
         mine = slot(h, rc, r)
         send(3, mine, mine, h, rc, h, x_peer)
@@ -334,6 +367,12 @@
 
         each(home.shape[1], body)
 
+        def ahead(q):
+            front[h, rc, q] = column(1, (q // fronts) * share2 + main2 + q % fronts)
+
+        each(n_col * fronts, ahead)
+
+    main2 = share2 - fronts
     last = n_col - 1
     upper = c // 2
     inner = c + upper * (last - 2 * c)
@@ -351,7 +390,7 @@
 
     def y_copy(i, p):
         return remote(
-            away.at[p, pl.ds(owner(i) * share2, share2)], y2_in.at[i, p],
+            away.at[p, pl.ds(owner(i) * share2, main2)], y2_in.at[i, p],
             send_y.at[i, p], recv_y.at[i, p], y_peer,
         )
 
@@ -384,79 +423,167 @@
             @pl.when(inner == 1)
             def _():
                 z_arrival(0, p)
-                each(share2, joined)
+                each(main2, joined)
 
             @pl.when(inner == 0)
             def _():
-                each(share2, plain)
+                each(main2, plain)
         else:
-            each(share2, plain)
+            each(main2, plain)
         z_copy(i, p).start()
+
+    def front_copy(i, h, p):
+        at = 3 * inner if i == 0 else i
+        return remote(
+            front_out.at[i, h, p], front_in.at[at, h, p],
+            send_f.at[i, h, p], recv_f.at[at, h, p], {"col": receiver(i)},
+        )
+
+    def front_arrival(at, h, p):
+        remote(
+            front_in.at[at, h, p], front_in.at[at, h, p],
+            send_f.at[0, h, p], recv_f.at[at, h, p], {"col": receiver(0)},
+        ).wait_recv()
+
+    def front_send(i, h, p):
+        def put(with_arrival):
+            for b in range(fronts):
+                value = front[h, p, owner(i) * fronts + b]
+                if with_arrival:
+                    value += front_in[0, h, p, b].astype(F32)
+                front_out[i, h, p, b] = value.astype(BF16)
+
+        if i == 2:
+            @pl.when(inner == 1)
+            def _():
+                front_arrival(0, h, p)
+                put(True)
+
+            @pl.when(inner == 0)
+            def _():
+                put(False)
+        else:
+            put(False)
+        front_copy(i, h, p).start()
+
+    def front_total(h, p, slots):
+        for at in slots:
+            front_arrival(at, h, p)
+        for b in range(fronts):
+            value = front[h, p, c * fronts + b]
+            for at in slots:
+                value += front_in[at, h, p, b].astype(F32)
+            if h:
+                front_y_out[p, b] = value.astype(BF16)
+            else:
+                front[h, p, c * fronts + b] = value
+
+    def by_place(work):
+        @pl.when(inner == 1)
+        def _():
+            work((1, 2, 3))
+
+        @pl.when(inner == 0)
+        def _():
+            work((1, 2))
+
+    def front_close(h, p):
+        by_place(functools.partial(front_total, h, p))
+        if h:
+            begin(remote(
+                front_y_out.at[p], front_y_in.at[p], send_fy.at[p], recv_fy.at[p], y_peer
+            ))
+
+    def put_out(p, b, value):
+        value = jnp.maximum(value + bias2_v[b:b + 1, :], 0.0)
+        out[p * size:(p + 1) * size, b * block:(b + 1) * block] = value.astype(BF16)
+
+    def front_finish(p):
+        arrived(front_y_in.at[p], send_fy.at[p], recv_fy.at[p])
+        for b in range(fronts):
+            put_out(p, main2 + b, front[0, p, c * fronts + b] + front_y_in[p, b].astype(F32))
 
     def finish(p, slots):
         for at in slots:
             z_arrival(at, p)
-        for b in range(share2):
+        for b in range(main2):
             value = home[p, c * share2 + b] + y2_in[last, p, b].astype(F32)
             for at in slots:
                 value += z_in[at, p, b].astype(F32)
-            value = jnp.maximum(value + bias2[b:b + 1, :], 0.0)
-            out[p * size:(p + 1) * size, b * block:(b + 1) * block] = value.astype(BF16)
-
-    load(w1, 0).wait()
+            put_out(p, b, value)
+
+    def finish_wait(p):
+        y_copy(last, p).wait_recv()
+
+    w1_load.wait()
     first_partial(0, 0)
     pass_on(0, 0)
+    pair(0, 0)
+    for part in range(1, parts):
+        hand_over(1, part)
+    for part in range(1, parts):
+        pass_on(0, part)
     first_partial(0, 1)
-    pass_on(0, 1)
-    pair(0, 0)
-    pair(0, 1)
     pass_on(1, 0)
-    pass_on(1, 1)
     passed(0)
     first_partial(1, 0)
     pair(1, 0)
+    along_y(1, 0)
+    pair(0, 1)
+    for part in range(1, parts):
+        pass_on(1, part)
+    arrived(live_in, live_sem.at[0], live_sem.at[1])
+    along_x(1, 0)
     passed(1)
     first_partial(1, 1)
-    load(w2, 1).start()
-    arrived(live_in, live_sem.at[0], live_sem.at[1])
-    along_y(1, 0)
+    along_y(0, 0)
+    forward(1, 0)
     pair(1, 1)
+    w2_load.wait()
+    second_partial(1, 0)
+    for i in range(n_col):
+        y_copy(i, 0).start()
+    front_send(0, 1, 0)
+    front_send(1, 1, 0)
+    along_x(0, 0)
     along_y(1, 1)
-    along_x(1, 0)
-    along_x(1, 1)
-    forward(1, 0)
-    along_y(0, 0)
-    load(w2, 1).wait()
-    second_partial(1, 0)
-    y_copy(0, 0).start()
-    forward(1, 1)
-    along_x(0, 0)
-    second_partial(1, 1)
-    y_copy(0, 1).start()
-    for i in range(1, n_col):
-        for p in range(2):
-            y_copy(i, p).start()
     along_y(0, 1)
     forward(0, 0)
     second_partial(0, 0)
+    along_x(1, 1)
+    along_z(0, 0)
+    front_send(0, 0, 0)
+    front_send(1, 0, 0)
     along_x(0, 1)
-    along_z(0, 0)
+    front_send(2, 1, 0)
+    along_z(1, 0)
+    forward(1, 1)
+    second_partial(1, 1)
+    for i in range(n_col):
+        y_copy(i, 1).start()
+    along_z(2, 0)
+    front_send(0, 1, 1)
+    front_send(1, 1, 1)
+    front_send(2, 0, 0)
     forward(0, 1)
     second_partial(0, 1)
+    front_send(0, 0, 1)
+    front_send(1, 0, 1)
     along_z(0, 1)
-    for i in range(1, last):
-        for p in range(2):
-            along_z(i, p)
-    for p in range(2):
-        y_copy(last, p).wait_recv()
-
-        @pl.when(inner == 1)
-        def _():
-            finish(p, (1, 2, 3))
-
-        @pl.when(inner == 0)
-        def _():
-            finish(p, (1, 2))
+    front_send(2, 1, 1)
+    front_send(2, 0, 1)
+    front_close(1, 0)
+    along_z(1, 1)
+    finish_wait(0)
+    by_place(functools.partial(finish, 0))
+    front_close(1, 1)
+    front_close(0, 0)
+    along_z(2, 1)
+    front_close(0, 1)
+    front_finish(0)
+    finish_wait(1)
+    by_place(functools.partial(finish, 1))
+    front_finish(1)
     for copy in started:
         copy.wait_send()
     for i in range(n_col):
@@ -464,6 +591,8 @@
             y_copy(i, p).wait_send()
             if i < last:
                 z_copy(i, p).wait_send()
+                front_copy(i, 0, p).wait_send()
+                front_copy(i, 1, p).wait_send()
 
 
 def fused_layers(acts, act_mask, w1, cols1, bias1, mask2, w2, cols2, bias2):
@@ -472,32 +601,42 @@
     rows = acts.shape[0]
     row_blocks, col_blocks = act_mask.shape[1], mask2.shape[1]
     n_row, n_col = lax.axis_size("row"), lax.axis_size("col")
-    r, d = lax.axis_index("row"), lax.axis_index("depth")
     size = rows // 2
     share1 = col_blocks // 2 // n_row
     share2 = row_blocks // n_col
-    staged, live_own, live_give, plan = prepare(acts, act_mask, cols1, cols2, mask2, block)
-    first = d * (col_blocks // 2) + r * share1
-    bias_part = lax.dynamic_slice_in_dim(bias1.reshape(col_blocks, block), first, share1, 0)
+    fronts = share2 // 8
     flat1, flat2 = w1.reshape(-1, block, block), w2.reshape(-1, block, block)
     count = flat1.shape[0]
     half = col_blocks // 2
-    smem = pl.BlockSpec(memory_space=pltpu.SMEM)
+    parts = 4
     vmem = pl.BlockSpec(memory_space=pltpu.VMEM)
-    hbm = pl.BlockSpec(memory_space=pl.ANY)
+    hbm = pl.BlockSpec(memory_space=pltpu.HBM)
     tile = (size, block)
     dma = pltpu.SemaphoreType.DMA
     return pl.pallas_call(
-        functools.partial(layers_kernel, n_col),
+        functools.partial(layers_kernel, n_col, fronts),
         out_shape=jax.ShapeDtypeStruct((rows, share2 * block), BF16),
-        in_specs=[smem] + [vmem] * 5 + [hbm] * 2,
+        in_specs=[hbm] * 9,
         out_specs=vmem,
         scratch_shapes=[
+            pltpu.VMEM((count, block, block), BF16),
             pltpu.VMEM((count, block, block), BF16),
             pltpu.VMEM((count + 1, *tile), F32),
             pltpu.VMEM((stored, *tile), BF16),
             pltpu.VMEM((stored, *tile), BF16),
-            pltpu.VMEM((rows, 128), BF16),
+            pltpu.VMEM((2, size, stored * block), BF16),
+            pltpu.VMEM((2, size, stored // 2 * block), BF16),
+            pltpu.VMEM((2, stored, *tile), BF16),
+            pltpu.VMEM((2, stored // 2, *tile), BF16),
+            pltpu.VMEM((row_blocks, rows), jnp.int32),
+            pltpu.VMEM(cols1.shape[::-1], jnp.int32),
+            pltpu.VMEM(cols2.shape[::-1], jnp.int32),
+            pltpu.VMEM((col_blocks, rows), jnp.int32),
+            pltpu.VMEM((col_blocks, block), F32),
+            pltpu.VMEM((share2, block), F32),
+            pltpu.VMEM((8, count), jnp.int32),
+            pltpu.SMEM((8, count), jnp.int32),
+            pltpu.VMEM((share1, rows), jnp.int32),
             pltpu.VMEM((2, 2, half, *tile), F32),
             pltpu.VMEM((2, 2, half, *tile), BF16),
             pltpu.VMEM((2, 2, half, *tile), BF16),
@@ -511,12 +650,17 @@
             pltpu.VMEM((half, *tile), BF16),
             pltpu.VMEM((2, row_blocks, *tile), BF16),
             pltpu.VMEM((2, row_blocks, *tile), F32),
-            pltpu.VMEM((n_col, 2, share2, *tile), BF16),
-            pltpu.VMEM((n_col - 1, 2, share2, *tile), BF16),
-            pltpu.VMEM((n_col, 2, share2, *tile), BF16),
-            dma((2,)),
-            dma((2, 2, 2)),
-            dma((2, 2, 2)),
+            pltpu.VMEM((n_col, 2, share2 - fronts, *tile), BF16),
+            pltpu.VMEM((n_col - 1, 2, share2 - fronts, *tile), BF16),
+            pltpu.VMEM((n_col, 2, share2 - fronts, *tile), BF16),
+            pltpu.VMEM((2, 2, n_col * fronts, *tile), F32),
+            pltpu.VMEM((n_col - 1, 2, 2, fronts, *tile), BF16),
+            pltpu.VMEM((n_col, 2, 2, fronts, *tile), BF16),
+            pltpu.VMEM((2, fronts, *tile), BF16),
+            pltpu.VMEM((2, fronts, *tile), BF16),
+            dma((16,)),
+            dma((2, 2, parts)),
+            dma((2, 2, parts)),
             dma((2,)),
             dma((6, 2, 2)),
             dma((6, 2, 2)),
@@ -524,12 +668,19 @@
             dma((n_col, 2)),
             dma((n_col - 1, 2)),
             dma((n_col, 2)),
+            dma((n_col - 1, 2, 2)),
+            dma((n_col, 2, 2)),
+            dma((2,)),
+            dma((2,)),
         ],
         compiler_params=pltpu.CompilerParams(
-            collective_id=1, has_side_effects=True, vmem_limit_bytes=60 * 1024 * 1024
+            collective_id=1, has_side_effects=True, vmem_limit_bytes=62 * 1024 * 1024
         ),
         name="layers",
-    )(plan, staged, live_own, live_give, bias_part, bias2.reshape(share2, block), flat1, flat2)
+    )(
+        acts, act_mask.T, cols1.T, cols2.T, mask2.T, bias1.reshape(col_blocks, block),
+        bias2.reshape(share2, block), flat1, flat2,
+    )
 
 
 def solution(mesh):

time: 118 us -> 93.1 us (0.79)
  Pallas kernels: 108 us -> 91.1 us
  local copies, waits for them, and re-layouts: 8.93 us -> 1.88 us
    pallas_call x2 -> x1, Pallas kernels: 108 us -> 91.1 us  [fused_layers(): pl.pallas_call(functools.partial(layers_kernel, n_col, fronts), out_shape...]
    unnamed x7 -> x1, local copies, waits for them, and re-layouts: 8.34 us -> 1.88 us
where the time goes in v2:
time: 93.1 us; the launch traced here: 93 us
  Pallas kernels  91.1 us (98%)
  local copies, waits for them, and re-layouts  1.88 us (2%)
    pallas_call x1, Pallas kernels, fused_layers(): pl.pallas_call(functools.partial(layers_kernel, n_col, fronts), out_shape...  91.1 us
    unnamed x1, local copies, waits for them, and re-layouts  1.88 us

profile of v2, /device:TPU:0, one launch (start us, length us, event | category | flops | bytes accessed | tf_op | source)
XLA Modules:
  0.0 93.0 jit_solution(18058805162877992927)
XLA Ops:
  0.0 91.1 %layers.1 = bf16[128,2048]{1,0:T(8,128)(2,1)} custom-call(bf16[128,8192]{1,0:T(8,128)(2,1)} %acts.1, s32[64,128]{1,0:T(8,128)} %bitcast.10, s32[8,64]{1,0:T(8,128)} %bitcast.14, s32[8,64]{1,0:T(8,128)} %bitcast.15, s32[64,128]{1,0:T(8,128)} %bitcast.11, f32[64,128]{1,0:T(8,128)} %bitcast.12, f32[16,128]{1,0:T(8,128)} %bitcast.13, ...), custom_call_target="tpu_custom_call" | custom-call | tf_op jit(solution)/shard_map/layers/pallas_call | solution.py:616
  91.1 1.9 %copy.11 = bf16[128,2048]{1,0:T(8,128)(2,1)} copy(bf16[128,2048]{1,0:T(8,128)(2,1)} %layers.1) | data formatting | bytes 1048576

commit v3 on v2

--- a/solution.py
+++ b/solution.py
@@ -261,7 +261,7 @@
 
     sums[entries] = jnp.zeros(sums.shape[1:], F32)
 
-    def multiply(x_ref, layer):
+    def multiply(x_ref, layer, between):
         weights = wbuf2 if layer else wbuf
         width = 64 if entries % 64 == 0 else 1
 
@@ -276,13 +276,17 @@
                 sums[p] = running
             return running
 
-        lax.fori_loop(0, entries // width, step, jnp.zeros(sums.shape[1:], F32))
+        steps = entries // width
+        running = lax.fori_loop(0, steps // 2, step, jnp.zeros(sums.shape[1:], F32))
+        if between is not None:
+            between()
+        lax.fori_loop(steps // 2, steps, step, running)
 
     def column(layer, b):
         return sums[plan[layer * 4 + 3, b]]
 
-    def first_partial(h, rc):
-        multiply(acts_in[rc] if h else keep.at[rc], 0)
+    def first_partial(h, rc, between=None):
+        multiply(acts_in[rc] if h else keep.at[rc], 0, between)
 
         def split(q):
             at = (q // share1) * 2 * share1 + q % share1
@@ -354,10 +358,10 @@
         await_stage(3, theirs, h, rc)
         send(5, theirs, theirs, h, rc, h, partner)
 
-    def second_partial(h, rc):
+    def second_partial(h, rc, between=None):
         await_stage(4, slot(h, rc, x * 2 + 1 - core), h, rc)
         await_stage(5, slot(h, rc, (1 - x) * 2 + 1 - core), h, rc)
-        multiply(x1[h][rc], 1)
+        multiply(x1[h][rc], 1, between)
 
         def body(b):
             if h:
@@ -368,11 +372,16 @@
         each(home.shape[1], body)
 
         def ahead(q):
-            front[h, rc, q] = column(1, (q // fronts) * share2 + main2 + q % fronts)
-
-        each(n_col * fronts, ahead)
-
-    main2 = share2 - fronts
+            front[h, q] = column(1, (q // fronts) * share2 + mains[0] + q % fronts)
+
+        if rc == 0:
+            each(n_col * fronts, ahead)
+
+    mains = (share2 - fronts, share2)
+
+    def main(ref, i, p):
+        return ref.at[i, p, pl.ds(0, mains[p])]
+
     last = n_col - 1
     upper = c // 2
     inner = c + upper * (last - 2 * c)
@@ -390,20 +399,20 @@
 
     def y_copy(i, p):
         return remote(
-            away.at[p, pl.ds(owner(i) * share2, main2)], y2_in.at[i, p],
+            away.at[p, pl.ds(owner(i) * share2, mains[p])], main(y2_in, i, p),
             send_y.at[i, p], recv_y.at[i, p], y_peer,
         )
 
     def z_copy(i, p):
         at = 3 * inner if i == 0 else i
         return remote(
-            z_out.at[i, p], z_in.at[at, p], send_z.at[i, p], recv_z.at[at, p],
+            main(z_out, i, p), main(z_in, at, p), send_z.at[i, p], recv_z.at[at, p],
             {"col": receiver(i)},
         )
 
     def z_arrival(at, p):
         remote(
-            z_in.at[at, p], z_in.at[at, p], send_z.at[0, p], recv_z.at[at, p],
+            main(z_in, at, p), main(z_in, at, p), send_z.at[0, p], recv_z.at[at, p],
             {"col": receiver(0)},
         ).wait_recv()
 
@@ -423,40 +432,40 @@
             @pl.when(inner == 1)
             def _():
                 z_arrival(0, p)
-                each(main2, joined)
+                each(mains[p], joined)
 
             @pl.when(inner == 0)
             def _():
-                each(main2, plain)
+                each(mains[p], plain)
         else:
-            each(main2, plain)
+            each(mains[p], plain)
         z_copy(i, p).start()
 
-    def front_copy(i, h, p):
+    def front_copy(i, h):
         at = 3 * inner if i == 0 else i
         return remote(
-            front_out.at[i, h, p], front_in.at[at, h, p],
-            send_f.at[i, h, p], recv_f.at[at, h, p], {"col": receiver(i)},
+            front_out.at[i, h], front_in.at[at, h],
+            send_f.at[i, h], recv_f.at[at, h], {"col": receiver(i)},
         )
 
-    def front_arrival(at, h, p):
+    def front_arrival(at, h):
         remote(
-            front_in.at[at, h, p], front_in.at[at, h, p],
-            send_f.at[0, h, p], recv_f.at[at, h, p], {"col": receiver(0)},
+            front_in.at[at, h], front_in.at[at, h],
+            send_f.at[0, h], recv_f.at[at, h], {"col": receiver(0)},
         ).wait_recv()
 
-    def front_send(i, h, p):
+    def front_send(i, h):
         def put(with_arrival):
             for b in range(fronts):
-                value = front[h, p, owner(i) * fronts + b]
+                value = front[h, owner(i) * fronts + b]
                 if with_arrival:
-                    value += front_in[0, h, p, b].astype(F32)
-                front_out[i, h, p, b] = value.astype(BF16)
+                    value += front_in[0, h, b].astype(F32)
+                front_out[i, h, b] = value.astype(BF16)
 
         if i == 2:
             @pl.when(inner == 1)
             def _():
-                front_arrival(0, h, p)
+                front_arrival(0, h)
                 put(True)
 
             @pl.when(inner == 0)
@@ -464,19 +473,19 @@
                 put(False)
         else:
             put(False)
-        front_copy(i, h, p).start()
-
-    def front_total(h, p, slots):
+        front_copy(i, h).start()
+
+    def front_total(h, slots):
         for at in slots:
-            front_arrival(at, h, p)
+            front_arrival(at, h)
         for b in range(fronts):
-            value = front[h, p, c * fronts + b]
+            value = front[h, c * fronts + b]
             for at in slots:
-                value += front_in[at, h, p, b].astype(F32)
+                value += front_in[at, h, b].astype(F32)
             if h:
-                front_y_out[p, b] = value.astype(BF16)
+                front_y_out[b] = value.astype(BF16)
             else:
-                front[h, p, c * fronts + b] = value
+                front[h, c * fronts + b] = value
 
     def by_place(work):
         @pl.when(inner == 1)
@@ -487,26 +496,24 @@
         def _():
             work((1, 2))
 
-    def front_close(h, p):
-        by_place(functools.partial(front_total, h, p))
+    def front_close(h):
+        by_place(functools.partial(front_total, h))
         if h:
-            begin(remote(
-                front_y_out.at[p], front_y_in.at[p], send_fy.at[p], recv_fy.at[p], y_peer
-            ))
+            begin(remote(front_y_out, front_y_in, send_fy.at[0], recv_fy.at[0], y_peer))
 
     def put_out(p, b, value):
         value = jnp.maximum(value + bias2_v[b:b + 1, :], 0.0)
         out[p * size:(p + 1) * size, b * block:(b + 1) * block] = value.astype(BF16)
 
-    def front_finish(p):
-        arrived(front_y_in.at[p], send_fy.at[p], recv_fy.at[p])
+    def front_finish():
+        arrived(front_y_in, send_fy.at[0], recv_fy.at[0])
         for b in range(fronts):
-            put_out(p, main2 + b, front[0, p, c * fronts + b] + front_y_in[p, b].astype(F32))
+            put_out(0, mains[0] + b, front[0, c * fronts + b] + front_y_in[b].astype(F32))
 
     def finish(p, slots):
         for at in slots:
             z_arrival(at, p)
-        for b in range(main2):
+        for b in range(mains[p]):
             value = home[p, c * share2 + b] + y2_in[last, p, b].astype(F32)
             for at in slots:
                 value += z_in[at, p, b].astype(F32)
@@ -535,55 +542,44 @@
     arrived(live_in, live_sem.at[0], live_sem.at[1])
     along_x(1, 0)
     passed(1)
-    first_partial(1, 1)
-    along_y(0, 0)
+    first_partial(1, 1, lambda: along_y(0, 0))
     forward(1, 0)
     pair(1, 1)
     w2_load.wait()
-    second_partial(1, 0)
+    second_partial(1, 0, lambda: along_x(0, 0))
     for i in range(n_col):
         y_copy(i, 0).start()
-    front_send(0, 1, 0)
-    front_send(1, 1, 0)
-    along_x(0, 0)
+    front_send(0, 1)
+    front_send(1, 1)
     along_y(1, 1)
     along_y(0, 1)
     forward(0, 0)
+    front_send(2, 1)
     second_partial(0, 0)
     along_x(1, 1)
     along_z(0, 0)
-    front_send(0, 0, 0)
-    front_send(1, 0, 0)
+    front_send(0, 0)
     along_x(0, 1)
-    front_send(2, 1, 0)
     along_z(1, 0)
     forward(1, 1)
     second_partial(1, 1)
     for i in range(n_col):
         y_copy(i, 1).start()
     along_z(2, 0)
-    front_send(0, 1, 1)
-    front_send(1, 1, 1)
-    front_send(2, 0, 0)
+    front_send(1, 0)
+    front_close(1)
     forward(0, 1)
     second_partial(0, 1)
-    front_send(0, 0, 1)
-    front_send(1, 0, 1)
+    front_send(2, 0)
     along_z(0, 1)
-    front_send(2, 1, 1)
-    front_send(2, 0, 1)
-    front_close(1, 0)
-    along_z(1, 1)
     finish_wait(0)
     by_place(functools.partial(finish, 0))
-    front_close(1, 1)
-    front_close(0, 0)
+    along_z(1, 1)
+    front_close(0)
     along_z(2, 1)
-    front_close(0, 1)
-    front_finish(0)
     finish_wait(1)
+    front_finish()
     by_place(functools.partial(finish, 1))
-    front_finish(1)
     for copy in started:
         copy.wait_send()
     for i in range(n_col):
@@ -591,8 +587,7 @@
             y_copy(i, p).wait_send()
             if i < last:
                 z_copy(i, p).wait_send()
-                front_copy(i, 0, p).wait_send()
-                front_copy(i, 1, p).wait_send()
+                front_copy(i, p).wait_send()
 
 
 def fused_layers(acts, act_mask, w1, cols1, bias1, mask2, w2, cols2, bias2):
@@ -604,7 +599,7 @@
     size = rows // 2
     share1 = col_blocks // 2 // n_row
     share2 = row_blocks // n_col
-    fronts = share2 // 8
+    fronts = share2 // 4
     flat1, flat2 = w1.reshape(-1, block, block), w2.reshape(-1, block, block)
     count = flat1.shape[0]
     half = col_blocks // 2
@@ -650,14 +645,14 @@
             pltpu.VMEM((half, *tile), BF16),
             pltpu.VMEM((2, row_blocks, *tile), BF16),
             pltpu.VMEM((2, row_blocks, *tile), F32),
-            pltpu.VMEM((n_col, 2, share2 - fronts, *tile), BF16),
-            pltpu.VMEM((n_col - 1, 2, share2 - fronts, *tile), BF16),
-            pltpu.VMEM((n_col, 2, share2 - fronts, *tile), BF16),
-            pltpu.VMEM((2, 2, n_col * fronts, *tile), F32),
-            pltpu.VMEM((n_col - 1, 2, 2, fronts, *tile), BF16),
-            pltpu.VMEM((n_col, 2, 2, fronts, *tile), BF16),
-            pltpu.VMEM((2, fronts, *tile), BF16),
-            pltpu.VMEM((2, fronts, *tile), BF16),
+            pltpu.VMEM((n_col, 2, share2, *tile), BF16),
+            pltpu.VMEM((n_col - 1, 2, share2, *tile), BF16),
+            pltpu.VMEM((n_col, 2, share2, *tile), BF16),
+            pltpu.VMEM((2, n_col * fronts, *tile), F32),
+            pltpu.VMEM((n_col - 1, 2, fronts, *tile), BF16),
+            pltpu.VMEM((n_col, 2, fronts, *tile), BF16),
+            pltpu.VMEM((fronts, *tile), BF16),
+            pltpu.VMEM((fronts, *tile), BF16),
             dma((16,)),
             dma((2, 2, parts)),
             dma((2, 2, parts)),
@@ -668,10 +663,10 @@
             dma((n_col, 2)),
             dma((n_col - 1, 2)),
             dma((n_col, 2)),
-            dma((n_col - 1, 2, 2)),
-            dma((n_col, 2, 2)),
-            dma((2,)),
-            dma((2,)),
+            dma((n_col - 1, 2)),
+            dma((n_col, 2)),
+            dma((1,)),
+            dma((1,)),
         ],
         compiler_params=pltpu.CompilerParams(
             collective_id=1, has_side_effects=True, vmem_limit_bytes=62 * 1024 * 1024

time: 93.1 us -> 90.2 us (0.969)
  Pallas kernels: 91.1 us -> 88.1 us
    pallas_call x1, Pallas kernels: 91.1 us -> 88.1 us  [fused_layers(): pl.pallas_call(functools.partial(layers_kernel, n_col, fronts), out_shape...]
where the time goes in v3:
time: 90.2 us; the launch traced here: 90 us
  Pallas kernels  88.1 us (98%)
  local copies, waits for them, and re-layouts  1.88 us (2%)
    pallas_call x1, Pallas kernels, fused_layers(): pl.pallas_call(functools.partial(layers_kernel, n_col, fronts), out_shape...  88.1 us
    unnamed x1, local copies, waits for them, and re-layouts  1.88 us

profile of v3, /device:TPU:0, one launch (start us, length us, event | category | flops | bytes accessed | tf_op | source)
XLA Modules:
  0.0 90.0 jit_solution(4318276939976206561)
XLA Ops:
  0.0 88.1 %layers.1 = bf16[128,2048]{1,0:T(8,128)(2,1)} custom-call(bf16[128,8192]{1,0:T(8,128)(2,1)} %acts.1, s32[64,128]{1,0:T(8,128)} %bitcast.10, s32[8,64]{1,0:T(8,128)} %bitcast.14, s32[8,64]{1,0:T(8,128)} %bitcast.15, s32[64,128]{1,0:T(8,128)} %bitcast.11, f32[64,128]{1,0:T(8,128)} %bitcast.12, f32[16,128]{1,0:T(8,128)} %bitcast.13, ...), custom_call_target="tpu_custom_call" | custom-call | tf_op jit(solution)/shard_map/layers/pallas_call | solution.py:611
  88.1 1.9 %copy.11 = bf16[128,2048]{1,0:T(8,128)(2,1)} copy(bf16[128,2048]{1,0:T(8,128)(2,1)} %layers.1) | data formatting | bytes 1048576

commit v4 on v3

--- a/solution.py
+++ b/solution.py
@@ -118,11 +118,11 @@
     n_col, fronts, acts, act_mask, cols1, cols2, mask2, bias1, bias2, w1, w2, out,
     wbuf, wbuf2, sums, acts_in0, acts_in1, keep_raw, give_raw, keep, give,
     act_mask_v, cols1_v, cols2_v, mask2_v, bias1_v, bias2_v, plan_v, plan, live_in,
-    kept, given, core_in, y_out, y_in, x_out, x_in,
+    kept, given, core_in, y_out, y_in, x_out, x_in, xf_out, xf_in,
     x1_00, x1_01, x1_10, x1_11, away, home, y2_in, z_out, z_in,
     front, front_out, front_in, front_y_out, front_y_in,
     load_sem, acts_send, acts_recv, live_sem, send_sem, recv_sem,
-    send_y, recv_y, send_z, recv_z, send_f, recv_f, send_fy, recv_fy,
+    send_y, recv_y, send_z, recv_z, send_f, recv_f, send_fy, recv_fy, xf_send, xf_recv,
 ):
     r, c, d = lax.axis_index("row"), lax.axis_index("col"), lax.axis_index("depth")
     n_row = lax.axis_size("row")
@@ -263,7 +263,7 @@
 
     def multiply(x_ref, layer, between):
         weights = wbuf2 if layer else wbuf
-        width = 64 if entries % 64 == 0 else 1
+        width = 128 if entries % 128 == 0 else 1
 
         def step(at, running):
             for u in range(width):
@@ -277,10 +277,12 @@
             return running
 
         steps = entries // width
-        running = lax.fori_loop(0, steps // 2, step, jnp.zeros(sums.shape[1:], F32))
+        half_way = steps // 2 if between is not None else 0
+        running = jnp.zeros(sums.shape[1:], F32)
         if between is not None:
+            running = lax.fori_loop(0, half_way, step, running)
             between()
-        lax.fori_loop(steps // 2, steps, step, running)
+        lax.fori_loop(half_way, steps, step, running)
 
     def column(layer, b):
         return sums[plan[layer * 4 + 3, b]]
@@ -321,6 +323,60 @@
         each(half, other)
         send(1, y_out.at[h, rc], y_in.at[1 - h, rc], h, rc, 1 - h, y_peer)
         each(half, own)
+
+    def pair_x():
+        await_stage(0, core_in.at[0, 1], 0, 1)
+        for side in (1 - d, d):
+            def theirs(q):
+                at = side * half + (1 - x) * quarter + q
+                xf_out[side, q] = (kept[0, 1, at] + core_in[0, 1, at].astype(F32)).astype(BF16)
+
+            each(quarter, theirs)
+        side_send(1 - d, 0)
+        for side in (1 - d, d):
+            def mine(q):
+                at = side * half + x * quarter + q
+                kept[0, 1, at] = kept[0, 1, at] + core_in[0, 1, at].astype(F32)
+
+            each(quarter, mine)
+
+    def side_send(side, n):
+        begin(remote(xf_out.at[side], xf_in.at[side], xf_send.at[n], xf_recv.at[n], x_peer))
+
+    def other_part(row):
+        return y_in.at[1, 1, pl.ds(row * quarter, quarter)]
+
+    def settle_other():
+        arrived(xf_in.at[1 - d], xf_send.at[0], xf_recv.at[0])
+
+        def body(q):
+            y_out[0, 1, q] = (
+                kept[0, 1, (1 - d) * half + x * quarter + q] + xf_in[1 - d, q].astype(F32)
+            ).astype(BF16)
+
+        each(quarter, body)
+        send(1, y_out.at[0, 1, pl.ds(0, quarter)], other_part(x), 0, 1, 1, y_peer)
+
+    def settle_own():
+        arrived(xf_in.at[d], xf_send.at[1], xf_recv.at[1])
+
+        def body(q):
+            at = d * half + x * quarter + q
+            kept[0, 1, at] = kept[0, 1, at] + xf_in[d, q].astype(F32)
+
+        each(quarter, body)
+
+    def cross_1():
+        def body(q):
+            x_out[1, 1, q] = kept[1, 1, d * half + (1 - x) * quarter + q].astype(BF16)
+
+        each(quarter, body)
+        send(2, x_out.at[1, 1], x_in.at[1, 1], 1, 1, 1, x_peer)
+
+    def cross_0():
+        await_stage(1, y_in.at[0, 1], 0, 1)
+        theirs = y_in.at[0, 1, pl.ds((1 - x) * quarter, quarter)]
+        send(2, theirs, x_in.at[0, 1], 0, 1, 0, x_peer)
 
     def along_y(h, rc):
         await_stage(1, y_in.at[h, rc], h, rc)
@@ -338,6 +394,8 @@
         return x1[h][rc].at[pl.ds(row * share1, share1)]
 
     def along_x(h, rc):
+        if (h, rc) == (1, 1):
+            await_stage(1, other_part(x), 1, 1)
         await_stage(2, x_in.at[h, rc], h, rc)
         live = (live_in if h else live_rows(d))[...].astype(F32).T[rc * size:(rc + 1) * size]
         shift = bias1_v[pl.ds(pl.multiple_of((d * n_row + r) * share1, share1), share1), :]
@@ -533,40 +591,42 @@
     first_partial(0, 1)
     pass_on(1, 0)
     passed(0)
-    first_partial(1, 0)
+    first_partial(1, 0, pair_x)
     pair(1, 0)
     along_y(1, 0)
-    pair(0, 1)
+    side_send(d, 1)
     for part in range(1, parts):
         pass_on(1, part)
+    settle_other()
     arrived(live_in, live_sem.at[0], live_sem.at[1])
     along_x(1, 0)
     passed(1)
     first_partial(1, 1, lambda: along_y(0, 0))
     forward(1, 0)
     pair(1, 1)
+    cross_1()
     w2_load.wait()
     second_partial(1, 0, lambda: along_x(0, 0))
     for i in range(n_col):
         y_copy(i, 0).start()
     front_send(0, 1)
     front_send(1, 1)
-    along_y(1, 1)
-    along_y(0, 1)
+    settle_own()
+    along_x(1, 1)
+    cross_0()
     forward(0, 0)
     front_send(2, 1)
     second_partial(0, 0)
-    along_x(1, 1)
     along_z(0, 0)
     front_send(0, 0)
     along_x(0, 1)
     along_z(1, 0)
+    front_send(1, 0)
     forward(1, 1)
     second_partial(1, 1)
     for i in range(n_col):
         y_copy(i, 1).start()
     along_z(2, 0)
-    front_send(1, 0)
     front_close(1)
     forward(0, 1)
     second_partial(0, 1)
@@ -599,7 +659,7 @@
     size = rows // 2
     share1 = col_blocks // 2 // n_row
     share2 = row_blocks // n_col
-    fronts = share2 // 4
+    fronts = share2 * 8 // 16
     flat1, flat2 = w1.reshape(-1, block, block), w2.reshape(-1, block, block)
     count = flat1.shape[0]
     half = col_blocks // 2
@@ -639,6 +699,8 @@
             pltpu.VMEM((2, 2, half // 2, *tile), BF16),
             pltpu.VMEM((2, 2, share1, *tile), BF16),
             pltpu.VMEM((2, 2, share1, *tile), BF16),
+            pltpu.VMEM((2, share1, *tile), BF16),
+            pltpu.VMEM((2, share1, *tile), BF16),
             pltpu.VMEM((half, *tile), BF16),
             pltpu.VMEM((half, *tile), BF16),
             pltpu.VMEM((half, *tile), BF16),
@@ -667,6 +729,8 @@
             dma((n_col, 2)),
             dma((1,)),
             dma((1,)),
+            dma((2,)),
+            dma((2,)),
         ],
         compiler_params=pltpu.CompilerParams(
             collective_id=1, has_side_effects=True, vmem_limit_bytes=62 * 1024 * 1024

time: 90.2 us -> 88.5 us (0.981)
  Pallas kernels: 88.1 us -> 86.4 us
    pallas_call x1, Pallas kernels: 88.1 us -> 86.4 us  [fused_layers(): pl.pallas_call(functools.partial(layers_kernel, n_col, fronts), out_shape...]
where the time goes in v4:
time: 88.5 us; the launch traced here: 88.3 us
  Pallas kernels  86.4 us (98%)
  local copies, waits for them, and re-layouts  1.88 us (2%)
    pallas_call x1, Pallas kernels, fused_layers(): pl.pallas_call(functools.partial(layers_kernel, n_col, fronts), out_shape...  86.4 us
    unnamed x1, local copies, waits for them, and re-layouts  1.88 us

profile of v4, /device:TPU:0, one launch (start us, length us, event | category | flops | bytes accessed | tf_op | source)
XLA Modules:
  0.0 88.3 jit_solution(16640045396569848020)
XLA Ops:
  0.0 86.4 %layers.1 = bf16[128,2048]{1,0:T(8,128)(2,1)} custom-call(bf16[128,8192]{1,0:T(8,128)(2,1)} %acts.1, s32[64,128]{1,0:T(8,128)} %bitcast.10, s32[8,64]{1,0:T(8,128)} %bitcast.14, s32[8,64]{1,0:T(8,128)} %bitcast.15, s32[64,128]{1,0:T(8,128)} %bitcast.11, f32[64,128]{1,0:T(8,128)} %bitcast.12, f32[16,128]{1,0:T(8,128)} %bitcast.13, ...), custom_call_target="tpu_custom_call" | custom-call | tf_op jit(solution)/shard_map/layers/pallas_call | solution.py:671
  86.4 1.9 %copy.11 = bf16[128,2048]{1,0:T(8,128)(2,1)} copy(bf16[128,2048]{1,0:T(8,128)(2,1)} %layers.1) | data formatting | bytes 1048576
